TPU v7x, 128 devices: a whole 4x4x4 slice. The times are simulated.
128 devices in a mesh: dp: 8 (over y, core), tensor: 16 (over x, z).
Axes of the slice: x: 4, y: 4, z: 4, core: 2. Of those that a mesh axis runs over, the one named last changes fastest.
Arguments:
- inputs: bfloat16 [24576, 5120], P('dp', 'tensor'), may hold values from -6 to 6
- cotangent: bfloat16 [24576, 4096], P('dp', 'tensor'), may hold values from -192 to 192
- lengths: int32 [64], P('dp'), may hold values from 96 to 384
- momentum: float32 [8, 4096, 5120], P('dp', 'tensor'), may hold values from -26 to 26
- weight: bfloat16 [4096, 5120], P('tensor'), may hold values from -0.00039863586 to 0.00039863586
- right_factor: float32 [5120, 64], replicated, may hold values from -1 to 1
Outputs:
- new_weight: bfloat16 [4096, 5120], P('tensor')
- new_momentum: float32 [8, 4096, 5120], P('dp', 'tensor')
- new_right: float32 [5120, 64], replicated
Inputs may be any that keep to these rules, and one draw needn't show every extreme that they name: The first lengths[i] positions of block i are real tokens, the rest padding.
All inputs are finite; a program needn't handle non-finite values.
Results may differ from a plain program's by a relative error of at most 0.00045.
Values may be sent and summed in bfloat16 or wider, within the bound.
A program may use at most 128 MiB of HBM per device.

v0:
```python
import math

import jax
import jax.numpy as jnp
from jax import lax
from jax.sharding import PartitionSpec as P

EPS = 1e-06
MU = 0.95
LR = 0.02


def from_everyone(x, axis):
    devices = lax.axis_size(axis)
    return lax.all_to_all(jnp.broadcast_to(x[None], (devices, *x.shape)), axis, 0, 0, tiled=True)


def over_copies(x, axis):
    return from_everyone(x, axis).sum(axis=0)


def per_device(inputs, cotangent, lengths, momentum, weight, right_factor):
    hi = lax.Precision.HIGHEST
    contract = (((0,), (0,)), ((), ()))
    replicas = lax.axis_size("dp")
    block_len = inputs.shape[0] // lengths.shape[0]
    position = jnp.arange(block_len, dtype=jnp.int32)
    keep = (position[None, :] < lengths[:, None]).reshape(-1).astype(jnp.bfloat16)
    masked = inputs * keep[:, None]
    count = jnp.sum(lengths.astype(jnp.float32))
    grad = lax.dot_general(
        cotangent,
        lax.all_gather(masked, "tensor", axis=1, tiled=True),
        contract,
        preferred_element_type=jnp.float32,
    )
    both = momentum[0] + grad / count
    left = over_copies(jnp.dot(both, right_factor, precision=hi), "dp") / replicas
    gram = over_copies(jnp.dot(left.T, left, precision=hi), "tensor")
    factor = jnp.linalg.cholesky(gram)
    ortho = jax.scipy.linalg.solve_triangular(factor, left.T, lower=True).T
    term = lax.dot_general(both, ortho, contract, precision=hi) / replicas
    right = lax.psum(term, ("dp", "tensor"))
    squares = jnp.sum(right * right, axis=0)
    new_right = right * lax.rsqrt(squares + EPS)
    lowrank = jnp.dot(ortho, right.T, precision=hi)
    new_momentum = (both - (1.0 - MU) * lowrank)[None]
    rows_all = ortho.shape[0] * lax.axis_size("tensor")
    update = jnp.dot(ortho, new_right.T, precision=hi)
    new_weight = (
        weight.astype(jnp.float32) - LR * math.sqrt(rows_all / right.shape[0]) * update
    ).astype(jnp.bfloat16)
    return (new_weight, new_momentum, new_right)


def solution(mesh):
    placed = (
        P("dp", "tensor"),
        P("dp", "tensor"),
        P("dp"),
        P("dp", "tensor", None),
        P("tensor", None),
        P(),
    )
    return jax.shard_map(
        per_device,
        mesh=mesh,
        in_specs=placed,
        out_specs=(P("tensor", None), P("dp", "tensor", None), P()),
        check_vma=False,
    )
```

profile of v0, /device:TPU:1, one launch (start us, length us, event | category | flops | bytes accessed | tf_op | source)
XLA Modules:
  0.0 449.7 jit_solution(14454124653131563446)
XLA Ops:
  7.2 0.0 copy-start
  7.2 0.0 all-gather.2.cloned.1.call-start
  7.2 0.8 fusion.15
  8.1 3.0 broadcast_multiply_fusion
  11.0 0.0 all-gather.2.cloned.1.call-update
  11.1 0.0 copy-start.7
  11.1 0.0 all-reduce.2.cloned.1.call-start
  11.1 5.9 %copy.22 = f32[1,256,5120]{1,2,0:T(8,128)} copy(f32[1,256,5120]{2,1,0:T(8,128)} %param.9) | data formatting | bytes 10485760 | tf_op args[3]
  17.0 0.0 copy-done.7
  17.0 0.6 convert_reduce_fusion
  17.6 0.0 copy-start.6
  17.6 183.0 %all-gather.2.cloned.1.call-done = bf16[3072,5120]{0,1:T(8,128)(2,1)} async-done(((bf16[3072,320]{0,1:T(8,128)(2,1)}), bf16[3072,5120]{0,1:T(8,128)(2,1)}) %all-gather.2.cloned.1.call-update) | async-done | bytes 31457296 | tf_op jit(solution)/shard_map/all_gather | solution.py:33
  200.6 0.0 copy-done
  200.6 17.1 %fusion.5 = f32[256,5120]{0,1:T(8,128)S(1)} fusion(bf16[3072,5120]{0,1:T(8,128)(2,1)} %all-gather.2.cloned.1.call-done, bf16[3072,256]{1,0:T(8,128)(2,1)S(1)} %copy-done, f32[1,256,5120]{1,2,0:T(8,128)} %copy.22, f32[]{:T(128)} %convert_reduce_fusion), kind=kOutput, calls=%fused_computation.8 | convolution fusion | flops 8055685120 | bytes 43515908 | tf_op jit(solution)/shard_map/dot_general | solution.py:31
  217.7 0.0 copy-done.6
  217.7 0.0 copy-start.2
  217.7 3.2 fusion.18
  220.9 0.0 copy-done.2
  221.0 14.2 %all_to_all.10 = f32[8,256,64]{1,2,0:T(8,128)S(1)} all-to-all(f32[8,256,64]{1,2,0:T(8,128)S(1)} %broadcast_in_dim.7), channel_id=1, replica_groups=mesh['dp'=8,'tensor'=16] {'dp'}, dimensions={0} | all-to-all | bytes 1048576 | tf_op jit(solution)/shard_map/all_to_all | solution.py:15
  235.2 0.2 fusion.8
  235.5 0.3 reshape.40
  235.8 12.2 %all_to_all.11 = f32[16,1,4096]{2,1,0:T(1,128)S(1)} all-to-all(f32[16,1,4096]{2,1,0:T(1,128)S(1)} %reshape.40), channel_id=1, replica_groups=mesh['dp'=8,'tensor'=16] {'tensor'}, dimensions={0} | all-to-all | bytes 524288 | tf_op jit(solution)/shard_map/all_to_all | solution.py:15
  248.1 0.5 broadcast.66
  248.6 1.3 reduce.6
  249.8 0.2 reshape.41
  250.1 0.1 copy.23
  250.2 5.8 %cholesky.16 = f32[64,64]{1,0:T(8,128)S(1)} custom-call(f32[64,64]{1,0:T(8,128)S(1)} %fusion.12), custom_call_target="Cholesky" | custom-call | tf_op jit(solution)/shard_map/jit(cholesky)/cholesky | solution.py:40
  256.1 0.6 compare_reduce_fusion
  256.7 0.7 fusion.10
  257.4 4.9 %custom-call.7 = f32[1,64,64]{1,2,0:T(8,128)S(1)} custom-call(f32[1,64,64]{2,1,0:T(8,128)S(1)} %fusion.10), custom_call_target="InvertDiagBlocksLowerTriangular" | custom-call | tf_op jit(solution)/shard_map/jit(_solve_triangular)/triangular_solve | solution.py:41
  262.3 0.3 fusion.6
  262.6 8.7 %convolution_multiply_fusion.2 = f32[5120,64]{0,1:T(8,128)} fusion(f32[256,5120]{0,1:T(8,128)} %copy-done.2, f32[64,256]{1,0:T(8,128)S(1)} %fusion.6), kind=kOutput, calls=%fused_computation.9 | convolution fusion | flops 1006960640 | bytes 6619136 | tf_op jit(solution)/shard_map/dot_general | solution.py:42
  271.3 0.0 all-reduce.2.cloned.1.call-update
  271.3 146.8 %all-reduce.2.cloned.1.call-done = f32[5120,64]{0,1:T(8,128)} async-done(((f32[5120,64]{0,1:T(8,128)}), f32[5120,64]{0,1:T(8,128)}) %all-reduce.2.cloned.1.call-update) | async-done | bytes 1310736 | tf_op jit(solution)/shard_map/psum | solution.py:43
  418.1 1.5 multiply_reduce_fusion
  419.6 9.7 %fusion.2 = f32[1,256,5120]{1,2,0:T(8,128)} fusion(f32[256,5120]{0,1:T(8,128)} %copy-done.2, f32[64,256]{1,0:T(8,128)S(1)} %fusion.6, f32[5120,64]{0,1:T(8,128)} %all-reduce.2.cloned.1.call-done), kind=kOutput, calls=%fused_computation.4 | convolution fusion | flops 1009254400 | bytes 11862016 | tf_op jit(solution)/shard_map/dot_general | solution.py:46
  429.3 0.0 copy-start.3
  429.3 6.0 %copy.25 = f32[1,256,5120]{2,1,0:T(8,128)} copy(f32[1,256,5120]{1,2,0:T(8,128)} %fusion.2) | data formatting | bytes 10485760
  435.3 0.0 copy-done.3
  435.3 0.0 copy-start.5
  435.3 0.0 copy-start.1
  435.3 0.2 broadcast_multiply_fusion.1
  435.5 1.6 copy-done.5
  437.1 0.0 copy-start.4
  437.1 5.8 %fusion.3 = bf16[256,5120]{1,0:T(8,128)(2,1)} fusion(f32[64,256]{1,0:T(8,128)S(1)} %fusion.6, f32[5120,64]{0,1:T(8,128)S(1)} %broadcast_multiply_fusion.1, bf16[256,5120]{1,0:T(8,128)(2,1)S(1)} %copy-done.5), kind=kOutput, calls=%fused_computation.5 | convolution fusion | flops 1011875840 | bytes 6619136 | tf_op jit(solution)/shard_map/dot_general | solution.py:49
  442.9 0.0 copy-done.4
  442.9 0.0 copy-done.1
  (8 shorter events, 0.2 us)
Async XLA Ops:
  7.2 193.5 %copy-start = (bf16[3072,256]{1,0:T(8,128)(2,1)S(1)}, bf16[3072,256]{1,0:T(8,128)(2,1)}, u32[]{:S(2)}) copy-start(bf16[3072,256]{1,0:T(8,128)(2,1)} %param.7) | copy-start | bytes 4718596
  7.2 193.5 %all-gather.2.cloned.1.call-start = ((), (), s32[]{:S(2)}) async-start(), calls=%async_computation.2 | async-start | bytes 33423360 | tf_op jit(solution)/shard_map/all_gather | solution.py:33
  11.1 5.9 %copy-start.7 = (s32[8]{0:T(128)S(1)}, s32[8]{0:T(128)}, u32[]{:S(2)}) copy-start(s32[8]{0:T(128)} %param.8) | copy-start | bytes 100
  11.1 407.0 %all-reduce.2.cloned.1.call-start = ((), (), s32[]{:S(2)}) async-start(), calls=%async_computation.3 | async-start | bytes 2621440 | tf_op jit(solution)/shard_map/psum | solution.py:43
  17.6 200.1 %copy-start.6 = (f32[5120,64]{0,1:T(8,128)S(1)}, f32[5120,64]{0,1:T(8,128)}, u32[]{:S(2)}) copy-start(f32[5120,64]{0,1:T(8,128)} %param.11) | copy-start | bytes 3932164
  217.7 3.2 copy-start.2
  429.3 6.0 %copy-start.3 = (f32[5120,64]{0,1:T(8,128)S(1)}, f32[5120,64]{0,1:T(8,128)}, u32[]{:S(2)}) copy-start(f32[5120,64]{0,1:T(8,128)} %all-reduce.2.cloned.1.call-done) | copy-start | bytes 3932164
  435.3 1.7 copy-start.5
  435.3 7.6 %copy-start.1 = (bf16[3072,256]{1,0:T(8,128)(2,1)S(1)}, bf16[3072,256]{1,0:T(8,128)(2,1)}, u32[]{:S(2)}) copy-start(bf16[3072,256]{1,0:T(8,128)(2,1)} %param.7) | copy-start | bytes 4718596
  437.1 5.8 %copy-start.4 = (f32[5120,64]{0,1:T(8,128)}, f32[5120,64]{0,1:T(8,128)S(1)}, u32[]{:S(2)}) copy-start(f32[5120,64]{0,1:T(8,128)S(1)} %broadcast_multiply_fusion.1) | copy-start | bytes 3932164
Sparse Core Ops, SparseCore 0:
  11.2 189.4 all-gather.1
  271.4 146.6 all-reduce.1
where the time goes:
time: 450 us
  waiting for transfers between devices  330 us (73%)
  matrix products  44.9 us (10%)
  blocking collectives  26.5 us (6%)
  other arithmetic  19.5 us (4%)
  local copies, waits for them, and re-layouts  14.7 us (3%)
  between operations  14.2 us (3%)
    all_gather x1, waiting for transfers between devices, per_device(): lax.all_gather(masked, 'tensor', axis=1, tiled=True)  183 us
    psum x1, waiting for transfers between devices, per_device(): right = lax.psum(term, ('dp', 'tensor'))  147 us
    all_to_all x2, blocking collectives, from_everyone(): lax.all_to_all(jnp.broadcast_to(x[None], (devices, *x.shape)), axis, 0, 0...  26.5 us
    dot_general x1, matrix products, per_device(): lax.dot_general(cotangent, lax.all_gather(masked, 'tensor', axis=1, tiled...  17.1 us
    unnamed x20, local copies, waits for them, and re-layouts  14 us
    dot_general x1, matrix products, per_device(): lowrank = jnp.dot(ortho, right.T, precision=hi)  9.69 us
  transfers between devices with their start and end apart: 2, of which 2 were waited for; matrix products, arithmetic and copies ran while one was open for 1% of the time, Pallas kernels for 0%

commit v1 on v0

v1 whole, which is shorter than its diff:
```python
import functools
import math

import jax
import jax.numpy as jnp
from jax import lax
from jax.experimental import pallas as pl
from jax.experimental.pallas import tpu as pltpu
from jax.sharding import PartitionSpec as P

EPS = 1e-06
MU = 0.95
LR = 0.02

f32 = jnp.float32
bf16 = jnp.bfloat16
HI = lax.Precision.HIGHEST
VMEM = pltpu.VMEM
DMA = pltpu.SemaphoreType.DMA
CODES = 32767.0


def vspec():
    return pl.BlockSpec(memory_space=pltpu.VMEM)


def anyspec():
    return pl.BlockSpec(memory_space=pl.ANY)


def tensor_place():
    t = lax.axis_index("tensor")
    return lax.div(t, 4), lax.rem(t, 4)


def around(i, by):
    return lax.rem(i + by, 4)


def remote(src, dst, send, recv, where):
    return pltpu.make_async_remote_copy(
        src_ref=src,
        dst_ref=dst,
        send_sem=send,
        recv_sem=recv,
        device_id=where,
        device_id_type=pl.DeviceIdType.MESH,
    )


def greet(peers):
    barrier = pltpu.get_barrier_semaphore()
    for peer in peers:
        pl.semaphore_signal(barrier, inc=1, device_id=peer, device_id_type=pl.DeviceIdType.MESH)
    pl.semaphore_wait(barrier, len(peers))


def grad_kernel(
    cot, packed, inv, mom, rf, both, left_t,
    A, B, codes, scales, R, RS, p1, p2, rfv, left, sl, sa, ra, sb, rb, sc, ss, rc, rs,
):
    x, z = tensor_place()
    zl, zr, zo = around(z, 3), around(z, 1), around(z, 2)
    xl, xr, xo = around(x, 3), around(x, 1), around(x, 2)

    def at(xx, zz):
        return {"tensor": xx * 4 + zz}

    tok = cot.shape[0]
    ha, hb = tok // 2, packed.shape[0] // 2
    width = packed.shape[1] // 2
    rows = cot.shape[1]

    locals_ = [
        pltpu.make_async_copy(cot, A.at[z], sl.at[0]),
        pltpu.make_async_copy(packed, B.at[x], sl.at[1]),
        pltpu.make_async_copy(mom, both, sl.at[2]),
        pltpu.make_async_copy(rf, rfv, sl.at[3]),
    ]
    greet([at(x, zl), at(x, zr), at(x, zo), at(xl, z), at(xr, z)])

    def part_a(h):
        return pl.ds(h * ha, ha)

    def part_b(h):
        return pl.ds(h * hb, hb)

    sent = []
    for half, right in ((0, True), (1, False), (1, True), (0, False)):
        k = half + (0 if right else 2)
        ca = remote(cot.at[part_a(half)], A.at[z, part_a(half)], sa.at[k], ra.at[k], at(x, zr if right else zl))
        ca.start()
        cb = remote(packed.at[part_b(half)], B.at[x, part_b(half)], sb.at[k], rb.at[k], at(xr if right else xl, z))
        cb.start()
        sent += [ca, cb]
    for c in locals_:
        c.start()

    def got_a(k):
        remote(A.at[z, part_a(0)], A.at[z, part_a(0)], sa.at[k], ra.at[k], at(x, zr)).wait_recv()

    def got_b(k):
        remote(B.at[x, part_b(0)], B.at[x, part_b(0)], sb.at[0], rb.at[k], at(xr, z)).wait_recv()

    def pass_a(k, half, origin, to):
        c = remote(A.at[origin, part_a(half)], A.at[origin, part_a(half)], sa.at[k], ra.at[k], at(x, to))
        c.start()
        sent.append(c)

    def pass_b(k, half, origin, to):
        c = remote(B.at[origin, part_b(half)], B.at[origin, part_b(half)], sb.at[k], rb.at[k], at(to, z))
        c.start()
        sent.append(c)

    got_a(0)
    pass_a(4, 0, zl, zr)
    got_a(3)
    pass_a(5, 1, zr, zl)
    got_b(0)
    pass_b(4, 0, xl, xr)
    got_b(3)
    pass_b(5, 1, xr, xl)

    pair0 = lax.div(x, 2)
    odd = lax.rem(x, 2)
    scale_in = inv[0]
    depth = 256

    def unit(i, carry):
        j, s = lax.div(i, 4), lax.rem(i, 4)
        ends = jnp.where(s == 0, 0, 2)
        ends = jnp.where(j == 0, ends, 2 - ends)
        off = jnp.where(s == 1, 3, jnp.where(s == 2, 1, ends))
        zz = around(z, off)
        pair = jnp.where(j == 0, pair0, 1 - pair0)

        @pl.when(i == 0)
        def _():
            locals_[0].wait()
            locals_[1].wait()
            got_b(2 - odd)

        @pl.when(i == 1)
        def _():
            got_a(1)

        @pl.when(i == 2)
        def _():
            got_a(2)

        @pl.when(i == 3)
        def _():
            got_a(4)
            got_a(5)

        @pl.when(i == 4)
        def _():
            got_b(1 + odd)
            got_b(4)
            got_b(5)

        p1[...] = jnp.zeros_like(p1)
        p2[...] = jnp.zeros_like(p2)

        def step(k, c):
            low = pl.ds(pl.multiple_of(k * depth, depth), depth)
            high = pl.ds(pl.multiple_of(ha + k * depth, depth), depth)
            a_low = A[zz, low, :]
            a_high = A[zz, high, :]
            for e in range(2):
                xx = pair * 2 + e
                p1[e] += lax.dot_general(
                    a_low, B[xx, low, 0:384], (((0,), (0,)), ((), ())), preferred_element_type=f32
                )
                p2[e] += lax.dot_general(
                    a_high, B[xx, low, 256:640], (((0,), (0,)), ((), ())), preferred_element_type=f32
                )
            return c

        lax.fori_loop(0, ha // depth, step, 0)
        p1[0] = p1[0] + pltpu.roll(p2[0], 384 - 64, 1)
        p1[1] = p2[1] + pltpu.roll(p1[1], 64, 1)
        low_lane = lax.broadcasted_iota(jnp.int32, (rows, 128), 1) < 64
        own = off == 0
        parts = (
            (0, 256, lambda: p1[0, :, 0:256]),
            (256, 128, lambda: jnp.where(low_lane, p1[0, :, 256:384], p1[1, :, 0:128])),
            (384, 256, lambda: p1[1, :, 128:384]),
        )
        for start, size, value in parts:
            v = value() * scale_in
            top = jnp.max(jnp.abs(v), axis=0, keepdims=True)
            live = top > 1e-30
            code = jnp.round(v * jnp.where(live, CODES / jnp.where(live, top, 1.0), 0.0))
            code = code.astype(jnp.int32).astype(jnp.int16)
            back = jnp.broadcast_to(jnp.where(live, top, 0.0) * (1.0 / CODES), (8, size))
            lanes = slice(start, start + size)

            @pl.when(own)
            def _():
                R[pair, z, :, lanes] = code
                RS[pair, z, :, lanes] = back

            @pl.when(jnp.logical_not(own))
            def _():
                codes[i, :, lanes] = code
                scales[i, :, lanes] = back

        @pl.when(jnp.logical_not(own))
        def _():
            remote(codes.at[i], R.at[pair, z], sc.at[i], rc.at[pair, z], at(x, zz)).start()
            remote(scales.at[i], RS.at[pair, z], ss.at[i], rs.at[pair, z], at(x, zz)).start()

        return carry

    lax.fori_loop(0, 8, unit, 0)
    locals_[2].wait()
    locals_[3].wait()
    left[...] = jnp.zeros_like(left)
    low_lane = lax.broadcasted_iota(jnp.int32, (64, 128), 1) < 64
    for j in range(2):
        pair = pair0 if j == 0 else 1 - pair0
        for by in (1, 3, 2):
            zz = around(z, by)
            remote(codes.at[0], R.at[pair, zz], sc.at[0], rc.at[pair, zz], at(x, zz)).wait_recv()
            remote(scales.at[0], RS.at[pair, zz], ss.at[0], rs.at[pair, zz], at(x, zz)).wait_recv()
        for e in range(2):
            for h in range(2):
                base = pl.multiple_of((pair * 2 + e) * 4 * width + h * 2 * width, 640)

                def piece(zz, r):
                    lanes = slice(0, 384) if e == 0 else slice(256, 640)
                    v = R[pair, zz, r, lanes].astype(jnp.int32).astype(f32) * RS[pair, zz, 0:1, lanes]
                    if zz % 2 == 0 and e == 1:
                        v = pltpu.roll(v, 384 - 64, 1)
                    if zz % 2 == 1 and e == 0:
                        v = pltpu.roll(v, 64, 1)
                    return v

                def chunk(q, c):
                    r = pl.ds(pl.multiple_of(q * 64, 64), 64)
                    first, second = piece(2 * h, r), piece(2 * h + 1, r)
                    both[r, pl.ds(base, 256)] += first[:, 0:256]
                    both[r, pl.ds(pl.multiple_of(base + 256, 128), 128)] += jnp.where(
                        low_lane, first[:, 256:384], second[:, 0:128]
                    )
                    both[r, pl.ds(pl.multiple_of(base + 384, 128), 256)] += second[:, 128:384]
                    return c

                lax.fori_loop(0, rows // 64, chunk, 0)
                left[...] += jnp.dot(
                    both[:, pl.ds(base, 640)], rfv[pl.ds(base, 640), :], precision=HI, preferred_element_type=f32
                )
    left_t[...] = left[...].T
    for c in sent:
        c.wait_send()
    for i in range(1, 7):
        remote(codes.at[i], R.at[0, 0], sc.at[i], rc.at[0, 0], at(x, zr)).wait_send()
        remote(scales.at[i], RS.at[0, 0], ss.at[i], rs.at[0, 0], at(x, zr)).wait_send()


def gradient(cot, packed, inv, mom, rf):
    tok, rows = cot.shape
    cols = mom.shape[1]
    rank = rf.shape[1]
    return pl.pallas_call(
        grad_kernel,
        out_shape=(
            jax.ShapeDtypeStruct((rows, cols), f32),
            jax.ShapeDtypeStruct((rank, rows), f32),
        ),
        in_specs=[anyspec(), anyspec(), pl.BlockSpec(memory_space=pltpu.SMEM), anyspec(), anyspec()],
        out_specs=(vspec(), vspec()),
        scratch_shapes=[
            VMEM((4, tok, rows), bf16),
            VMEM((4,) + packed.shape, bf16),
            VMEM((8, rows, 640), jnp.int16),
            VMEM((8, 8, 640), f32),
            VMEM((2, 4, rows, 640), jnp.int16),
            VMEM((2, 4, 8, 640), f32),
            VMEM((2, rows, 384), f32),
            VMEM((2, rows, 384), f32),
            VMEM((cols, rank), f32),
            VMEM((rows, rank), f32),
            DMA((4,)), DMA((6,)), DMA((6,)), DMA((6,)), DMA((6,)),
            DMA((8,)), DMA((8,)), DMA((2, 4)), DMA((2, 4)),
        ],
        compiler_params=pltpu.CompilerParams(collective_id=0, has_side_effects=True),
        name="grad2d",
    )(cot, packed, inv, mom, rf)


def sums_kernel(
    part, both, out, left_out, gram_out,
    L0, L1, T, D, P1, P2, P3, G1, G2, send, recv,
):
    x, z = tensor_place()
    d = lax.axis_index("dp")
    y, c = lax.div(d, 2), lax.rem(d, 2)
    place = {"x": x, "y": y, "z": z}

    def at(axis, k):
        if axis == "core":
            return {"dp": y * 2 + k}
        if axis == "y":
            return {"dp": k * 2 + c}
        if axis == "x":
            return {"tensor": k * 4 + z}
        return {"tensor": x * 4 + k}

    mate = at("core", 1 - c)
    greet([mate] + [at(a, around(place[a], q)) for a in "xyz" for q in (1, 2, 3)])
    pending = []

    def swap(stage, src, dst):
        copy = remote(src, dst, send.at[stage, 0], recv.at[stage, 0], mate)
        copy.start()
        pending.append(copy)
        return copy

    def spread(stage, axis, src, dst):
        me = place[axis]
        waits = []
        for q in (2, 1, 3):
            k = around(me, q)
            copy = remote(src(k), dst(me), send.at[stage, q], recv.at[stage, q], at(axis, k))
            copy.start()
            pending.append(copy)
            waits.append(remote(src(k), dst(around(me, 4 - q)), send.at[stage, q], recv.at[stage, q], at(axis, k)))

        def wait():
            for w in waits:
                w.wait_recv()

        return wait

    swap(0, part, L0).wait_recv()
    L1[y] = part[...] + L0[...]
    spread(1, "y", lambda k: L1.at[y], lambda k: L1.at[k])()
    left = (L1[0] + L1[1] + L1[2] + L1[3]) * (1.0 / 8.0)
    left_out[...] = left
    gram = lax.dot_general(left, left, (((1,), (1,)), ((), ())), precision=HI, preferred_element_type=f32)
    G1[z] = gram
    gram_wait = spread(2, "z", lambda k: G1.at[z], lambda k: G1.at[k])

    tiles = both.shape[1] // 128
    half = tiles * 8 // 2

    def block(g, carry):
        cols = pl.ds(pl.multiple_of(g * 640, 640), 640)
        v = jnp.dot(left_out[...], both[:, cols], precision=HI, preferred_element_type=f32)
        for i in range(5):
            T[pl.ds(g * 40 + i * 8, 8)] = v[:, 128 * i : 128 * (i + 1)].reshape(8, 8, 128)
        return carry

    lax.fori_loop(4 * (1 - c), 4 * (1 - c) + 4, block, 0)
    mine, theirs = c * half, (1 - c) * half
    core_wait = swap(3, T.at[pl.ds(theirs, half)], D)
    lax.fori_loop(4 * c, 4 * c + 4, block, 0)
    core_wait.wait_recv()

    def add_core(g, carry):
        r = pl.ds(mine + g * 20, 20)
        T[r] = T[r] + D[pl.ds(g * 20, 20)]
        return carry

    lax.fori_loop(0, half // 20, add_core, 0)

    n1, n2 = half // 8, half // 32
    orders = (("y", "x", "z"), ("x", "z", "y"))
    base = [mine + k * (half // 2) for k in range(2)]
    waits = []
    for k, (a1, a2, a3) in enumerate(orders):
        waits.append(
            spread(
                4 + k, a1,
                lambda q, k=k: T.at[pl.ds(base[k] + q * n1, n1)],
                lambda q, k=k: P1.at[k, q],
            )
        )
    first, second = [], []
    for k, (a1, a2, a3) in enumerate(orders):
        me = place[a1]
        P1[k, me] = T[pl.ds(base[k] + me * n1, n1)]
        waits[k]()
        P1[k, 0] = P1[k, 0] + P1[k, 1] + P1[k, 2] + P1[k, 3]
        first.append(
            spread(
                6 + k, a2,
                lambda q, k=k: P1.at[k, 0, pl.ds(q * n2, n2)],
                lambda q, k=k: P2.at[k, q],
            )
        )
    gram_wait()
    G2[x] = G1[0] + G1[1] + G1[2] + G1[3]
    gram_wait = spread(8, "x", lambda k: G2.at[x], lambda k: G2.at[k])
    for k, (a1, a2, a3) in enumerate(orders):
        me = place[a2]
        P2[k, me] = P1[k, 0, pl.ds(me * n2, n2)]
        first[k]()
        m3 = place[a3]
        P3[k, m3] = P2[k, 0] + P2[k, 1] + P2[k, 2] + P2[k, 3]
        second.append(spread(9 + k, a3, lambda q, k=k, m3=m3: P3.at[k, m3], lambda q, k=k: P3.at[k, q]))
    gram_wait()
    gram_out[...] = G2[0] + G2[1] + G2[2] + G2[3]
    third, fourth = [], []
    for k, (a1, a2, a3) in enumerate(orders):
        second[k]()
        row = base[k] + place[a1] * n1
        spot = row + place[a2] * n2
        out[pl.ds(spot, n2)] = P3[k, 0] + P3[k, 1] + P3[k, 2] + P3[k, 3]
        third.append(
            spread(
                11 + k, a2,
                lambda q, spot=spot: out.at[pl.ds(spot, n2)],
                lambda q, row=row: out.at[pl.ds(row + q * n2, n2)],
            )
        )
    for k, (a1, a2, a3) in enumerate(orders):
        third[k]()
        row = base[k] + place[a1] * n1
        fourth.append(
            spread(
                13 + k, a1,
                lambda q, row=row: out.at[pl.ds(row, n1)],
                lambda q, k=k: out.at[pl.ds(base[k] + q * n1, n1)],
            )
        )
    fourth[0]()
    fourth[1]()
    swap(15, out.at[pl.ds(mine, half)], out.at[pl.ds(mine, half)])
    remote(out.at[pl.ds(theirs, half)], out.at[pl.ds(theirs, half)], send.at[15, 0], recv.at[15, 0], mate).wait_recv()
    for copy in pending:
        copy.wait_send()


def sums(part, both):
    rank, rows = part.shape
    tiles = both.shape[1] // 128 * (rank // 8)
    half = tiles // 2
    n1, n2 = half // 8, half // 32
    return pl.pallas_call(
        sums_kernel,
        out_shape=(
            jax.ShapeDtypeStruct((tiles, 8, 128), f32),
            jax.ShapeDtypeStruct((rank, rows), f32),
            jax.ShapeDtypeStruct((rank, rank), f32),
        ),
        in_specs=[vspec(), vspec()],
        out_specs=(vspec(), vspec(), vspec()),
        scratch_shapes=[
            VMEM((rank, rows), f32),
            VMEM((4, rank, rows), f32),
            VMEM((tiles, 8, 128), f32),
            VMEM((half, 8, 128), f32),
            VMEM((2, 4, n1, 8, 128), f32),
            VMEM((2, 4, n2, 8, 128), f32),
            VMEM((2, 4, n2, 8, 128), f32),
            VMEM((4, rank, rank), f32),
            VMEM((4, rank, rank), f32),
            DMA((16, 4)),
            DMA((16, 4)),
        ],
        compiler_params=pltpu.CompilerParams(collective_id=1, has_side_effects=True),
        name="sums",
    )(part, both)


def finish_kernel(coef, total, linv, left_t, both, weight, new_weight, new_mom, new_right, RT, O2, N):
    step = pl.program_id(0)

    @pl.when(step == 0)
    def _():
        sq = jnp.zeros((RT.shape[0], 128), f32)

        def col(j, sq):
            v = jnp.dot(linv[...], total[j], precision=HI, preferred_element_type=f32) * (1.0 / 8.0)
            RT[:, pl.ds(pl.multiple_of(j * 128, 128), 128)] = v
            return sq + v * v

        sq = lax.fori_loop(0, total.shape[0], col, sq)
        norm = lax.rsqrt(jnp.sum(sq, axis=1, keepdims=True) + EPS)
        N[...] = jnp.broadcast_to(norm, N.shape)
        ortho_t = jnp.dot(linv[...], left_t[...], precision=HI, preferred_element_type=f32)
        rows = ortho_t.shape[1]
        O2[0:rows, :] = (ortho_t * (1.0 - MU)).T
        O2[rows : 2 * rows, :] = (ortho_t * norm * coef).T

    rows = both.shape[0]
    rt = RT[:, pl.ds(pl.multiple_of(step * 640, 640), 640)]
    low = jnp.dot(O2[...], rt, precision=HI, preferred_element_type=f32)
    new_mom[...] = both[...] - low[0:rows]
    new_weight[...] = (weight[...].astype(f32) - low[rows:]).astype(bf16)
    new_right[...] = (rt * N[:, 0:1]).T


def finish(coef, total, linv, left_t, both, weight):
    rows, cols = both.shape
    rank = linv.shape[0]
    whole = lambda *shape: pl.BlockSpec(shape, lambda i: (0,) * len(shape))
    blocked = pl.BlockSpec((rows, 640), lambda i: (0, i))
    return pl.pallas_call(
        functools.partial(finish_kernel, coef),
        grid=(cols // 640,),
        out_shape=(
            jax.ShapeDtypeStruct((rows, cols), bf16),
            jax.ShapeDtypeStruct((rows, cols), f32),
            jax.ShapeDtypeStruct((cols, rank), f32),
        ),
        in_specs=[whole(*total.shape), whole(rank, rank), whole(rank, rows), blocked, blocked],
        out_specs=(blocked, blocked, pl.BlockSpec((640, rank), lambda i: (i, 0))),
        scratch_shapes=[VMEM((rank, cols), f32), VMEM((2 * rows, rank), f32), VMEM((rank, 128), f32)],
        name="finish",
    )(total, linv, left_t, both, weight)


def per_device(inputs, cotangent, lengths, momentum, weight, right_factor):
    block_len = inputs.shape[0] // lengths.shape[0]
    position = jnp.arange(block_len, dtype=jnp.int32)
    keep = (position[None, :] < lengths[:, None]).reshape(-1).astype(bf16)
    masked = inputs * keep[:, None]
    half = masked.shape[0] // 2
    packed = jnp.concatenate([masked[:half], masked[half:]], axis=1)
    inv = 1.0 / jnp.sum(lengths.astype(f32))
    both, part = gradient(cotangent, packed, inv.reshape(1), momentum[0], right_factor)
    total, left_t, gram = sums(part, both)
    factor = jnp.linalg.cholesky(gram)
    linv = jax.scipy.linalg.solve_triangular(factor, jnp.eye(gram.shape[0], dtype=f32), lower=True)
    rank = gram.shape[0]
    rows_all = both.shape[0] * lax.axis_size("tensor")
    coef = LR * math.sqrt(rows_all / both.shape[1])
    new_weight, new_mom, new_right = finish(
        coef, total.reshape(-1, rank, 128), linv, left_t, both, weight
    )
    return (new_weight, new_mom[None], new_right)


def solution(mesh):
    placed = (
        P("dp", "tensor"),
        P("dp", "tensor"),
        P("dp"),
        P("dp", "tensor", None),
        P("tensor", None),
        P(),
    )
    return jax.shard_map(
        per_device,
        mesh=mesh,
        in_specs=placed,
        out_specs=(P("tensor", None), P("dp", "tensor", None), P()),
        check_vma=False,
    )
```

time: 450 us -> 193 us (0.43)
  waiting for transfers between devices: 330 us -> 0 us
  Pallas kernels: 0 us -> 164 us
  matrix products: 44.9 us -> 0.85 us
  blocking collectives: 26.5 us -> 0 us
  between operations: 14.2 us -> 1.39 us
  local copies, waits for them, and re-layouts: 14.7 us -> 8.94 us
    all_gather x1 -> x0, waiting for transfers between devices: 183 us -> none  [per_device(): lax.all_gather(masked, 'tensor', axis=1, tiled=True)]
    pallas_call x0 -> x3, Pallas kernels: none -> 164 us  [the longest x1 99.2 us: gradient(): pl.pallas_call(grad_kernel, out_shape=(jax.ShapeDtypeStruct((rows, cols),...]
    psum x1 -> x0, waiting for transfers between devices: 147 us -> none  [per_device(): right = lax.psum(term, ('dp', 'tensor'))]
    dot_general x6 -> x0, matrix products: 44.6 us -> none  [the longest x1 17.1 us: per_device(): lax.dot_general(cotangent, lax.all_gather(masked, 'tensor', axis=1, tiled...]
    all_to_all x2 -> x0, blocking collectives: 26.5 us -> none  [from_everyone(): lax.all_to_all(jnp.broadcast_to(x[None], (devices, *x.shape)), axis, 0, 0...]
    unnamed x20 -> x5, local copies, waits for them, and re-layouts: 14 us -> 7.85 us
  transfers between devices with their start and end apart: 2 -> 0, of which waited for: 2 -> 0; matrix products, arithmetic and copies ran while one was open for 1% -> 0% of each run, Pallas kernels for 0% -> 0%
where the time goes in v1:
time: 193 us; the launch traced here: 192 us
  Pallas kernels  164 us (85%)
  other arithmetic  17.3 us (9%)
  local copies, waits for them, and re-layouts  8.94 us (5%)
    pallas_call x1, Pallas kernels, gradient(): pl.pallas_call(grad_kernel, out_shape=(jax.ShapeDtypeStruct((rows, cols),...  99.2 us
    pallas_call x1, Pallas kernels, sums(): pl.pallas_call(sums_kernel, out_shape=(jax.ShapeDtypeStruct((tiles, 8, 12...  43.8 us
    pallas_call x1, Pallas kernels, finish(): pl.pallas_call(functools.partial(finish_kernel, coef), grid=(cols // 640,...  20.6 us
    unnamed x5, local copies, waits for them, and re-layouts  7.85 us
    another operation x3, other arithmetic, per_device(): factor = jnp.linalg.cholesky(gram)  6.52 us
    another operation x2, other arithmetic, per_device(): jax.scipy.linalg.solve_triangular(factor, jnp.eye(gram.shape[0], dtype=f3...  5.55 us

profile of v1, /device:TPU:1, one launch (start us, length us, event | category | flops | bytes accessed | tf_op | source)
XLA Modules:
  0.0 192.1 jit_solution(2340314543371625872)
XLA Ops:
  0.6 1.3 convert_reduce_fusion
  2.6 0.7 fusion.4
  3.3 2.9 %copy.9 = bf16[3072,320]{1,0:T(8,128)(2,1)S(1)} copy(bf16[3072,320]{0,1:T(8,128)(2,1)} %param.6) | data formatting | bytes 3932160 | tf_op args[0]
  6.2 0.5 broadcast_multiply_fusion
  6.7 0.2 fusion.5
  7.0 0.0 copy-start
  7.0 2.0 %pad_maximum_fusion.packed = bf16[1536,640]{1,0:T(8,128)(2,1)} fusion(bf16[1536,320]{1,0:T(8,128)(2,1)S(1)} %get-tuple-element.23, bf16[1536,320]{1,0:T(8,128)(2,1)S(1)} %get-tuple-element.22), kind=kLoop, calls=%fused_computation | loop fusion | flops 3932160 | bytes 3932160 | tf_op jit(solution)/shard_map/concatenate | solution.py:523
  9.0 0.0 copy-done
  9.0 2.0 %copy.10.rf = f32[5120,64]{1,0:T(8,128)} copy(f32[5120,64]{0,1:T(8,128)S(1)} %copy-done) | data formatting | bytes 2621440 | tf_op args[5]
  11.0 99.2 %grad2d.1 = (f32[256,5120]{1,0:T(8,128)}, f32[64,256]{1,0:T(8,128)}) custom-call(bf16[3072,256]{1,0:T(8,128)(2,1)} %cot.1, bf16[1536,640]{1,0:T(8,128)(2,1)} %pad_maximum_fusion.packed, f32[1]{0:T(128)} %bitcast.inv, f32[256,5120]{1,0:T(8,128)} %bitcast.13, f32[5120,64]{1,0:T(8,128)} %copy.10.rf), custom_call_target="tpu_custom_call" | custom-call | tf_op jit(solution)/shard_map/grad2d/pallas_call | solution.py:266
  110.2 43.8 %sums.1 = (f32[320,8,128]{2,1,0:T(8,128)}, f32[64,256]{1,0:T(8,128)}, f32[64,64]{1,0:T(8,128)}) custom-call(f32[64,256]{1,0:T(8,128)} %get-tuple-element.11.part, f32[256,5120]{1,0:T(8,128)} %get-tuple-element.12.both), custom_call_target="tpu_custom_call" | custom-call | tf_op jit(solution)/shard_map/sums/pallas_call | solution.py:442
  154.0 0.8 copy.11
  154.8 0.8 fusion.3
  155.6 5.8 %cholesky.17 = f32[64,64]{1,0:T(8,128)S(1)} custom-call(f32[64,64]{1,0:T(8,128)S(1)} %fusion.3), custom_call_target="Cholesky" | custom-call | tf_op jit(solution)/shard_map/jit(cholesky)/cholesky | solution.py:527
  161.5 0.6 compare_reduce_fusion
  162.1 0.7 fusion
  162.8 4.9 %custom-call.7 = f32[1,64,64]{1,2,0:T(8,128)S(1)} custom-call(f32[1,64,64]{2,1,0:T(8,128)S(1)} %fusion), custom_call_target="InvertDiagBlocksLowerTriangular" | custom-call | tf_op jit(solution)/shard_map/jit(_solve_triangular)/triangular_solve | solution.py:528
  167.7 0.8 fusion.1.linv
  168.5 20.6 %finish.1 = (bf16[256,5120]{1,0:T(8,128)(2,1)}, f32[256,5120]{1,0:T(8,128)}, f32[5120,64]{1,0:T(8,128)}) custom-call(f32[40,64,128]{2,1,0:T(8,128)} %bitcast.14, f32[64,64]{1,0:T(8,128)} %fusion.1.linv, f32[64,256]{1,0:T(8,128)} %get-tuple-element.15.left_t, f32[256,5120]{1,0:T(8,128)} %get-tuple-element.12.both, bf16[256,5120]{1,0:T(8,128)(2,1)} %weight.1), custom_call_target="tpu_custom_call" | custom-call | tf_op jit(solution)/shard_map/finish/pallas_call | solution.py:502
  189.2 2.9 %copy.12 = f32[5120,64]{0,1:T(8,128)} copy(f32[5120,64]{1,0:T(8,128)} %get-tuple-element.21) | data formatting | bytes 2621440
  (2 shorter events, 0.0 us)
Async XLA Ops:
  7.0 2.0 %copy-start = (f32[5120,64]{0,1:T(8,128)S(1)}, f32[5120,64]{0,1:T(8,128)}, u32[]{:S(2)}) copy-start(f32[5120,64]{0,1:T(8,128)} %param.11) | copy-start | bytes 3932164

commit v2 on v0

v2 whole, which is shorter than its diff:
```python
import functools
import math

import jax
import jax.numpy as jnp
from jax import lax
from jax.experimental import pallas as pl
from jax.experimental.pallas import tpu as pltpu
from jax.sharding import PartitionSpec as P

EPS = 1e-06
MU = 0.95
LR = 0.02

f32 = jnp.float32
bf16 = jnp.bfloat16
HI = lax.Precision.HIGHEST
VMEM = pltpu.VMEM
DMA = pltpu.SemaphoreType.DMA
CODES = 32767.0
DEPTH = 768


def vspec():
    return pl.BlockSpec(memory_space=pltpu.VMEM)


def anyspec():
    return pl.BlockSpec(memory_space=pl.ANY)


def sspec():
    return pl.BlockSpec(memory_space=pltpu.SMEM)


def around(i, by):
    return lax.rem(i + by, 4)


def cols_of(start, size):
    return pl.ds(pl.multiple_of(start, 128), size)


def split(v):
    high = v.astype(bf16)
    return high, (v - high.astype(f32)).astype(bf16)


def dot(a, b, contract=((1,), (0,))):
    return lax.dot_general(a, b, (contract, ((), ())), preferred_element_type=f32)


def remote(src, dst, send, recv, where):
    return pltpu.make_async_remote_copy(
        src_ref=src,
        dst_ref=dst,
        send_sem=send,
        recv_sem=recv,
        device_id=where,
        device_id_type=pl.DeviceIdType.MESH,
    )


def greet(peers):
    barrier = pltpu.get_barrier_semaphore()
    for peer in peers:
        pl.semaphore_signal(barrier, inc=1, device_id=peer, device_id_type=pl.DeviceIdType.MESH)
    pl.semaphore_wait(barrier, len(peers))


def comm_kernel(
    cot, bt, lengths, mom, rft, both_out, out, linv_out, left_out,
    A, B, codes, scales, R, RS, relay, relay_s, acc, keep, S, R2, both, rfv,
    LT, L0, L1, LL, T, D, P1, P2, P3, G1, G2, M,
    sl, sa, ra, sb, rb, sc, ss, rc, rs, sf, sfs, rf, rfs, send, recv,
):
    t = lax.axis_index("tensor")
    d = lax.axis_index("dp")
    x, z = lax.div(t, 4), lax.rem(t, 4)
    y, c = lax.div(d, 2), lax.rem(d, 2)
    place = {"x": x, "y": y, "z": z}

    def along(axis, k):
        if axis == "core":
            return {"dp": y * 2 + k}
        if axis == "y":
            return {"dp": k * 2 + c}
        if axis == "x":
            return {"tensor": k * 4 + z}
        return {"tensor": x * 4 + k}

    zl, zr, zo = around(z, 3), around(z, 1), around(z, 2)
    xl, xr, xo = around(x, 3), around(x, 1), around(x, 2)
    tok, rows = cot.shape
    feats = bt.shape[0]
    ha, hb = tok // 2, feats // 2
    mate = along("core", 1 - c)

    locals_ = [
        pltpu.make_async_copy(cot, A.at[z], sl.at[0]),
        pltpu.make_async_copy(bt, B.at[x], sl.at[1]),
        pltpu.make_async_copy(mom, both, sl.at[2]),
        pltpu.make_async_copy(rft, rfv, sl.at[3]),
    ]
    greet([mate] + [along(a, around(place[a], q)) for a in "xyz" for q in (1, 2, 3)])

    def part_a(h):
        return pl.ds(h * ha, ha)

    def part_b(h):
        return pl.ds(h * hb, hb)

    sent = []
    for half, right in ((0, True), (1, False), (1, True), (0, False)):
        k = half + (0 if right else 2)
        ca = remote(cot.at[part_a(half)], A.at[z, part_a(half)], sa.at[k], ra.at[k], along("z", zr if right else zl))
        ca.start()
        cb = remote(bt.at[part_b(half)], B.at[x, part_b(half)], sb.at[k], rb.at[k], along("x", xr if right else xl))
        cb.start()
        sent += [ca, cb]
    for copy in locals_:
        copy.start()

    def got_a(k):
        remote(A.at[z, part_a(0)], A.at[z, part_a(0)], sa.at[0], ra.at[k], along("z", zr)).wait_recv()

    def got_b(k):
        remote(B.at[x, part_b(0)], B.at[x, part_b(0)], sb.at[0], rb.at[k], along("x", xr)).wait_recv()

    def pass_a(k, half, origin, to):
        copy = remote(A.at[origin, part_a(half)], A.at[origin, part_a(half)], sa.at[k], ra.at[k], along("z", to))
        copy.start()
        sent.append(copy)

    def pass_b(k, half, origin, to):
        copy = remote(B.at[origin, part_b(half)], B.at[origin, part_b(half)], sb.at[k], rb.at[k], along("x", to))
        copy.start()
        sent.append(copy)

    block_len = tok // lengths.shape[0]
    count = lengths[0]
    for b in range(lengths.shape[0]):
        keep[:, b * block_len : (b + 1) * block_len] = (
            lax.broadcasted_iota(jnp.int32, (16, block_len), 1) < lengths[b]
        ).astype(f32).astype(bf16)
        if b:
            count = count + lengths[b]
    share = 1.0 / jnp.full((1, rows), count, jnp.int32).astype(f32)

    def unit(xx, zz, code_ref, scale_ref):
        acc[...] = jnp.zeros_like(acc)

        def step(k, carry):
            r = cols_of(k * DEPTH, DEPTH)
            acc[...] += dot(B[xx, :, r] * keep[0:1, r], A[zz, r, :])
            return carry

        lax.fori_loop(0, tok // DEPTH, step, 0)
        v = acc[...] * share
        top = jnp.max(jnp.abs(v), axis=0, keepdims=True)
        live = top > 1e-30
        code = jnp.round(v * jnp.where(live, CODES / jnp.where(live, top, 1.0), 0.0))
        code_ref[...] = code.astype(jnp.int32).astype(jnp.int16)
        scale_ref[...] = jnp.broadcast_to(jnp.where(live, top, 0.0) * (1.0 / CODES), (8, rows))

    def made(xx, zz):
        unit(xx, zz, codes.at[xx, zz], scales.at[xx, zz])

    def home(xx, zz):
        remote(codes.at[xx, zz], R.at[xx, z], sc.at[xx, zz], rc.at[xx, z], along("z", zz)).start()
        remote(scales.at[xx, zz], RS.at[xx, z], ss.at[xx, zz], rs.at[xx, z], along("z", zz)).start()

    def half_way(xx, side, n):
        to = along("z", around(z, jnp.where(side == 0, 1, 3)))
        remote(codes.at[xx, zo], relay.at[side, n], sc.at[xx, zo], rf.at[side, n], to).start()
        remote(scales.at[xx, zo], relay_s.at[side, n], ss.at[xx, zo], rfs.at[side, n], to).start()

    def hand_on(o, wait_only=False):
        side, n = o % 2, o // 2
        xx = (x, xl, xr, xo)[o]
        origin, to = (zl, zr) if side == 0 else (zr, zl)
        one = remote(relay.at[side, n], R.at[xx, origin], sf.at[side, n], rf.at[side, n], along("z", to))
        one.wait_recv()
        two = remote(relay_s.at[side, n], RS.at[xx, origin], sfs.at[side, n], rfs.at[side, n], along("z", to))
        two.wait_recv()
        remote(relay.at[side, n], R.at[xx, origin], sf.at[side, n], rc.at[xx, origin], along("z", to)).start()
        remote(relay_s.at[side, n], RS.at[xx, origin], sfs.at[side, n], rs.at[xx, origin], along("z", to)).start()

    locals_[0].wait()
    locals_[1].wait()
    unit(x, z, R.at[x, z], RS.at[x, z])
    locals_[2].wait()
    locals_[3].wait()
    rank = rft.shape[0]
    r_high, r_low = split(rfv[...])
    R2[0:rank] = r_high
    R2[rank : 2 * rank] = r_low
    LT[...] = jnp.zeros_like(LT)

    def mom_left(g, carry):
        r = cols_of(g * 256, 256)
        high, low = split(both[:, r])
        v = dot(R2[:, r], high, ((1,), (1,)))
        LT[...] += v[0:rank] + v[rank:] + dot(R2[0:rank, r], low, ((1,), (1,)))
        return carry

    lax.fori_loop(0, both.shape[1] // 256, mom_left, 0)

    got_a(0)
    pass_a(4, 0, zl, zr)
    got_a(3)
    pass_a(5, 1, zr, zl)
    got_b(0)
    pass_b(4, 0, xl, xr)
    got_b(3)
    pass_b(5, 1, xr, xl)
    got_a(1)
    got_a(2)

    def own_cols(i, carry):
        zz = around(z, 3 - 2 * i)
        made(x, zz)
        home(x, zz)
        return carry

    lax.fori_loop(0, 2, own_cols, 0)
    got_b(1)
    got_b(2)

    def next_cols(i, carry):
        xx = around(x, 3 - 2 * lax.div(i, 3))
        m = lax.rem(i, 3)

        @pl.when(m == 2)
        def _():
            unit(xx, z, R.at[xx, z], RS.at[xx, z])

        @pl.when(m != 2)
        def _():
            made(xx, around(z, 3 - 2 * m))

        return carry

    lax.fori_loop(0, 6, next_cols, 0)
    got_a(4)
    got_a(5)

    def far_rows(i, carry):
        xx = around(x, jnp.where(i == 0, 0, 5 - 2 * i))
        made(xx, zo)
        half_way(xx, lax.rem(i, 2), lax.div(i, 2))
        return carry

    lax.fori_loop(0, 3, far_rows, 0)
    for xx in (xl, xr):
        home(xx, zl)
        home(xx, zr)
    for o in range(3):
        hand_on(o)
    got_b(4)
    got_b(5)

    def far_cols(i, carry):
        @pl.when(i == 0)
        def _():
            made(xo, zo)
            half_way(xo, 1, 1)

        @pl.when(jnp.logical_and(i != 0, i != 3))
        def _():
            zz = around(z, 5 - 2 * i)
            made(xo, zz)
            home(xo, zz)

        @pl.when(i == 3)
        def _():
            unit(xo, z, R.at[xo, z], RS.at[xo, z])

        return carry

    lax.fori_loop(0, 4, far_cols, 0)
    hand_on(3)

    def gather_home(o, carry):
        xx = around(x, jnp.where(o == 0, 0, jnp.where(o == 3, 2, 5 - 2 * o)))
        for by in (1, 3, 2):
            zz = around(z, by)
            remote(codes.at[0, 0], R.at[xx, zz], sc.at[0, 0], rc.at[xx, zz], along("z", zz)).wait_recv()
            remote(scales.at[0, 0], RS.at[xx, zz], ss.at[0, 0], rs.at[xx, zz], along("z", zz)).wait_recv()
        for h in range(2):
            base = xx * (4 * feats) + h * (2 * feats)
            for i in range(2):
                S[i * feats : (i + 1) * feats] = R[xx, 2 * h + i].astype(jnp.int32).astype(f32) * RS[xx, 2 * h + i, 0:1]
            high, low = split(S[...])
            r = cols_of(base, 2 * feats)
            v = dot(R2[:, r], high)
            LT[...] += v[0:rank] + v[rank:] + dot(R2[0:rank, r], low)
            for i in range(2 * feats // 128):
                both[:, cols_of(base + 128 * i, 128)] += S[128 * i : 128 * (i + 1)].T
        return carry

    lax.fori_loop(0, 4, gather_home, 0)

    save = pltpu.make_async_copy(both, both_out, sl.at[4])
    save.start()
    pending = []

    def swap(stage, src, dst):
        copy = remote(src, dst, send.at[stage, 0], recv.at[stage, 0], mate)
        copy.start()
        pending.append(copy)
        return copy

    def spread(stage, axis, src, dst):
        me = place[axis]
        waits = []
        for q in (2, 1, 3):
            k = around(me, q)
            copy = remote(src(k), dst(me), send.at[stage, q], recv.at[stage, q], along(axis, k))
            copy.start()
            pending.append(copy)
            waits.append(remote(src(k), dst(around(me, 4 - q)), send.at[stage, q], recv.at[stage, q], along(axis, k)))

        def wait():
            for w in waits:
                w.wait_recv()

        return wait

    swap(0, LT, L0).wait_recv()
    L1[y] = LT[...] + L0[...]
    spread(1, "y", lambda k: L1.at[y], lambda k: L1.at[k])()
    left = (L1[0] + L1[1] + L1[2] + L1[3]) * (1.0 / 8.0)
    left_out[...] = left
    left_high, left_low = split(left)
    LL[0:rank] = left_high
    LL[rank : 2 * rank] = left_low
    v = dot(LL[...], left_high, ((1,), (1,)))
    G1[z] = v[0:rank] + v[rank:] + dot(left_high, left_low, ((1,), (1,)))
    gram_wait = spread(2, "z", lambda k: G1.at[z], lambda k: G1.at[k])

    tiles = both.shape[1] // 128 * (rank // 8)
    half = tiles // 2
    blocks = both.shape[1] // 512

    def block(g, carry):
        high, low = split(both[:, cols_of(g * 256, 256)])
        v = dot(LL[...], high)
        v = v[0:rank] + v[rank:] + dot(LL[0:rank], low)
        for i in range(2):
            T[pl.ds(g * 16 + i * 8, 8)] = v[:, 128 * i : 128 * (i + 1)].reshape(8, 8, 128)
        return carry

    lax.fori_loop(blocks * (1 - c), blocks * (2 - c), block, 0)
    mine, theirs = c * half, (1 - c) * half
    core_wait = swap(3, T.at[pl.ds(theirs, half)], D)
    lax.fori_loop(blocks * c, blocks * (1 + c), block, 0)
    core_wait.wait_recv()

    def add_core(g, carry):
        r = pl.ds(mine + g * 20, 20)
        T[r] = T[r] + D[pl.ds(g * 20, 20)]
        return carry

    lax.fori_loop(0, half // 20, add_core, 0)

    n1, n2 = half // 8, half // 32
    orders = (("y", "x", "z"), ("x", "z", "y"))
    base = [mine + k * (half // 2) for k in range(2)]
    zeroth, first, second, third, fourth = [], [], [], [], []
    for k, (a1, a2, a3) in enumerate(orders):
        zeroth.append(
            spread(
                4 + k, a1,
                lambda q, k=k: T.at[pl.ds(base[k] + q * n1, n1)],
                lambda q, k=k: P1.at[k, q],
            )
        )
    gram_wait()
    G2[x] = G1[0] + G1[1] + G1[2] + G1[3]
    gram_wait = spread(8, "x", lambda k: G2.at[x], lambda k: G2.at[k])
    for k, (a1, a2, a3) in enumerate(orders):
        me = place[a1]
        P1[k, me] = T[pl.ds(base[k] + me * n1, n1)]
        zeroth[k]()
        P1[k, 0] = P1[k, 0] + P1[k, 1] + P1[k, 2] + P1[k, 3]
        first.append(
            spread(
                6 + k, a2,
                lambda q, k=k: P1.at[k, 0, pl.ds(q * n2, n2)],
                lambda q, k=k: P2.at[k, q],
            )
        )
    row_id = lax.broadcasted_iota(jnp.int32, (rank, 2 * rank), 0)
    lane_id = lax.broadcasted_iota(jnp.int32, (rank, 2 * rank), 1)
    gram_wait()
    M[...] = jnp.where(lane_id == row_id + rank, 1.0, 0.0)
    M[:, 0:rank] = G2[0] + G2[1] + G2[2] + G2[3]

    def pivot(k, carry):
        m = M[...]
        row = M[pl.ds(k, 1), :]
        top = jnp.sum(jnp.where(lane_id[0:1] == k, row, 0.0), axis=1, keepdims=True)
        factor = jnp.sum(jnp.where(lane_id == k, m, 0.0), axis=1, keepdims=True)
        factor = jnp.where(row_id[:, 0:1] > k, factor / top, 0.0)
        M[...] = m - factor * row
        return carry

    cuts = (0, 16, 32, 48, rank)
    lax.fori_loop(cuts[0], cuts[1], pivot, 0)
    for k, (a1, a2, a3) in enumerate(orders):
        me = place[a2]
        P2[k, me] = P1[k, 0, pl.ds(me * n2, n2)]
        first[k]()
        m3 = place[a3]
        P3[k, m3] = P2[k, 0] + P2[k, 1] + P2[k, 2] + P2[k, 3]
        second.append(spread(9 + k, a3, lambda q, k=k, m3=m3: P3.at[k, m3], lambda q, k=k: P3.at[k, q]))
    lax.fori_loop(cuts[1], cuts[2], pivot, 0)
    for k, (a1, a2, a3) in enumerate(orders):
        second[k]()
        row = base[k] + place[a1] * n1
        spot = row + place[a2] * n2
        out[pl.ds(spot, n2)] = P3[k, 0] + P3[k, 1] + P3[k, 2] + P3[k, 3]
        third.append(
            spread(
                11 + k, a2,
                lambda q, spot=spot: out.at[pl.ds(spot, n2)],
                lambda q, row=row: out.at[pl.ds(row + q * n2, n2)],
            )
        )
    lax.fori_loop(cuts[2], cuts[3], pivot, 0)
    for k, (a1, a2, a3) in enumerate(orders):
        third[k]()
        row = base[k] + place[a1] * n1
        fourth.append(
            spread(
                13 + k, a1,
                lambda q, row=row: out.at[pl.ds(row, n1)],
                lambda q, k=k: out.at[pl.ds(base[k] + q * n1, n1)],
            )
        )
    lax.fori_loop(cuts[3], cuts[4], pivot, 0)
    m = M[...]
    diag = jnp.sum(jnp.where(lane_id == row_id, m, 0.0), axis=1, keepdims=True)
    linv_out[...] = pltpu.roll(m / jnp.sqrt(diag), rank, 1)[:, 0:rank]
    fourth[0]()
    fourth[1]()
    swap(15, out.at[pl.ds(mine, half)], out.at[pl.ds(mine, half)])
    remote(out.at[pl.ds(theirs, half)], out.at[pl.ds(theirs, half)], send.at[15, 0], recv.at[15, 0], mate).wait_recv()

    for copy in pending + sent:
        copy.wait_send()
    for by in (1, 2, 3):
        for xx in range(4):
            zz = around(z, by)
            remote(codes.at[xx, zz], R.at[0, 0], sc.at[xx, zz], rc.at[0, 0], along("z", zr)).wait_send()
            remote(scales.at[xx, zz], RS.at[0, 0], ss.at[xx, zz], rs.at[0, 0], along("z", zr)).wait_send()
    for o in range(4):
        side, n = o % 2, o // 2
        remote(relay.at[side, n], R.at[0, 0], sf.at[side, n], rc.at[0, 0], along("z", zr)).wait_send()
        remote(relay_s.at[side, n], RS.at[0, 0], sfs.at[side, n], rs.at[0, 0], along("z", zr)).wait_send()
    save.wait()


def communicate(cot, bt, lengths, mom, rft):
    tok, rows = cot.shape
    feats = bt.shape[0]
    rank, cols = rft.shape
    tiles = cols // 128 * (rank // 8)
    half = tiles // 2
    n1, n2 = half // 8, half // 32
    return pl.pallas_call(
        comm_kernel,
        out_shape=(
            jax.ShapeDtypeStruct((rows, cols), f32),
            jax.ShapeDtypeStruct((tiles, 8, 128), f32),
            jax.ShapeDtypeStruct((rank, rank), f32),
            jax.ShapeDtypeStruct((rank, rows), f32),
        ),
        in_specs=[anyspec(), anyspec(), sspec(), anyspec(), anyspec()],
        out_specs=(anyspec(), vspec(), vspec(), vspec()),
        scratch_shapes=[
            VMEM((4, tok, rows), bf16),
            VMEM((4, feats, tok), bf16),
            VMEM((4, 4, feats, rows), jnp.int16),
            VMEM((4, 4, 8, rows), f32),
            VMEM((4, 4, feats, rows), jnp.int16),
            VMEM((4, 4, 8, rows), f32),
            VMEM((2, 2, feats, rows), jnp.int16),
            VMEM((2, 2, 8, rows), f32),
            VMEM((feats, rows), f32),
            VMEM((16, tok), bf16),
            VMEM((2 * feats, rows), f32),
            VMEM((2 * rank, cols), bf16),
            VMEM((rows, cols), f32),
            VMEM((rank, cols), f32),
            VMEM((rank, rows), f32),
            VMEM((rank, rows), f32),
            VMEM((4, rank, rows), f32),
            VMEM((2 * rank, rows), bf16),
            VMEM((tiles, 8, 128), f32),
            VMEM((half, 8, 128), f32),
            VMEM((2, 4, n1, 8, 128), f32),
            VMEM((2, 4, n2, 8, 128), f32),
            VMEM((2, 4, n2, 8, 128), f32),
            VMEM((4, rank, rank), f32),
            VMEM((4, rank, rank), f32),
            VMEM((rank, 2 * rank), f32),
            DMA((5,)), DMA((6,)), DMA((6,)), DMA((6,)), DMA((6,)),
            DMA((4, 4)), DMA((4, 4)), DMA((4, 4)), DMA((4, 4)),
            DMA((2, 2)), DMA((2, 2)), DMA((2, 2)), DMA((2, 2)),
            DMA((16, 4)), DMA((16, 4)),
        ],
        compiler_params=pltpu.CompilerParams(collective_id=0, has_side_effects=True),
        name="communicate",
    )(cot, bt, lengths, mom, rft)


def finish_kernel(
    coef, total, linv, left_t, both, weight, new_weight, new_mom, new_right_t,
    bv, wv, RT, R3, O3, NR, isem, osem,
):
    rows, cols = both.shape
    rank = linv.shape[0]
    wide = cols // 8

    def fetch(i):
        r = cols_of(i * wide, wide)
        return (
            pltpu.make_async_copy(both.at[:, r], bv.at[:, r], isem.at[i, 0]),
            pltpu.make_async_copy(weight.at[:, r], wv.at[:, r], isem.at[i, 1]),
        )

    def store(i):
        r = cols_of(i * wide, wide)
        return (
            pltpu.make_async_copy(bv.at[:, r], new_mom.at[:, r], osem.at[i, 0]),
            pltpu.make_async_copy(wv.at[:, r], new_weight.at[:, r], osem.at[i, 1]),
        )

    for i in range(8):
        for copy in fetch(i):
            copy.start()
    l_high, l_low = split(linv[...] * (1.0 / 8.0))

    def col(j, sq):
        high, low = split(jnp.concatenate([total[2 * j], total[2 * j + 1]], axis=1))
        v = dot(l_high, high) + dot(l_low, high) + dot(l_high, low)
        r = cols_of(j * 256, 256)
        RT[:, r] = v
        v_high, v_low = split(v)
        R3[0:rank, r] = v_high
        R3[rank : 2 * rank, r] = v_low
        R3[2 * rank : 3 * rank, r] = v_high
        return sq + v * v

    sq = lax.fori_loop(0, cols // 256, col, jnp.zeros((rank, 256), f32))
    norm = lax.rsqrt(jnp.sum(sq, axis=1, keepdims=True) + EPS)
    NR[...] = RT[...] * norm
    tell = pltpu.make_async_copy(NR, new_right_t, osem.at[8, 0])
    tell.start()
    ortho_t = jnp.dot(linv[...], left_t[...], precision=HI, preferred_element_type=f32)
    both_t = jnp.concatenate([ortho_t * (1.0 - MU), ortho_t * (norm * coef)], axis=1)
    o_high, o_low = split(both_t)
    O3[...] = jnp.concatenate([o_high, o_high, o_low], axis=0).T

    def work(i, carry):
        for copy in fetch(i):
            copy.wait()
        r = cols_of(i * wide, wide)
        low = dot(O3[...], R3[:, r])
        bv[:, r] = bv[:, r] - low[0:rows]
        wv[:, r] = (wv[:, r].astype(f32) - low[rows:]).astype(bf16)
        for copy in store(i):
            copy.start()
        return carry

    lax.fori_loop(0, 8, work, 0)
    for i in range(8):
        for copy in store(i):
            copy.wait()
    tell.wait()


def finish(coef, total, linv, left_t, both, weight):
    rows, cols = both.shape
    rank = linv.shape[0]
    return pl.pallas_call(
        functools.partial(finish_kernel, coef),
        out_shape=(
            jax.ShapeDtypeStruct((rows, cols), bf16),
            jax.ShapeDtypeStruct((rows, cols), f32),
            jax.ShapeDtypeStruct((rank, cols), f32),
        ),
        in_specs=[vspec(), vspec(), vspec(), anyspec(), anyspec()],
        out_specs=(anyspec(), anyspec(), anyspec()),
        scratch_shapes=[
            VMEM((rows, cols), f32),
            VMEM((rows, cols), bf16),
            VMEM((rank, cols), f32),
            VMEM((3 * rank, cols), bf16),
            VMEM((2 * rows, 3 * rank), bf16),
            VMEM((rank, cols), f32),
            DMA((8, 2)),
            DMA((9, 2)),
        ],
        name="finish",
    )(total, linv, left_t, both, weight)


def per_device(inputs, cotangent, lengths, momentum, weight, right_factor):
    both, total, linv, left_t = communicate(cotangent, inputs.T, lengths, momentum[0], right_factor.T)
    rank = linv.shape[0]
    rows_all = both.shape[0] * lax.axis_size("tensor")
    coef = LR * math.sqrt(rows_all / both.shape[1])
    new_weight, new_mom, new_right_t = finish(
        coef, total.reshape(-1, rank, 128), linv, left_t, both, weight
    )
    return (new_weight, new_mom[None], new_right_t.T)


def solution(mesh):
    placed = (
        P("dp", "tensor"),
        P("dp", "tensor"),
        P("dp"),
        P("dp", "tensor", None),
        P("tensor", None),
        P(),
    )
    return jax.shard_map(
        per_device,
        mesh=mesh,
        in_specs=placed,
        out_specs=(P("tensor", None), P("dp", "tensor", None), P()),
        check_vma=False,
    )
```

time: 450 us -> 139 us (0.31)
  waiting for transfers between devices: 330 us -> 0 us
  Pallas kernels: 0 us -> 138 us
  matrix products: 44.9 us -> 0 us
  blocking collectives: 26.5 us -> 0 us
  other arithmetic: 19.5 us -> 0 us
  local copies, waits for them, and re-layouts: 14.7 us -> 0 us
  between operations: 14.2 us -> 0.64 us
    all_gather x1 -> x0, waiting for transfers between devices: 183 us -> none  [per_device(): lax.all_gather(masked, 'tensor', axis=1, tiled=True)]
    psum x1 -> x0, waiting for transfers between devices: 147 us -> none  [per_device(): right = lax.psum(term, ('dp', 'tensor'))]
    pallas_call x0 -> x2, Pallas kernels: none -> 138 us  [the longest x1 129 us: communicate(): pl.pallas_call(comm_kernel, out_shape=(jax.ShapeDtypeStruct((rows, cols),...]
    dot_general x6 -> x0, matrix products: 44.6 us -> none  [the longest x1 17.1 us: per_device(): lax.dot_general(cotangent, lax.all_gather(masked, 'tensor', axis=1, tiled...]
    all_to_all x2 -> x0, blocking collectives: 26.5 us -> none  [from_everyone(): lax.all_to_all(jnp.broadcast_to(x[None], (devices, *x.shape)), axis, 0, 0...]
    unnamed x20 -> x0, local copies, waits for them, and re-layouts: 14 us -> none
    another operation x5 -> x0, other arithmetic: 12.1 us -> none  [the longest x3 6.52 us: per_device(): factor = jnp.linalg.cholesky(gram)]
  transfers between devices with their start and end apart: 2 -> 0, of which waited for: 2 -> 0; matrix products, arithmetic and copies ran while one was open for 1% -> 0% of each run, Pallas kernels for 0% -> 0%
where the time goes in v2:
time: 139 us; the launch traced here: 138 us
  Pallas kernels  138 us (99%)
    pallas_call x1, Pallas kernels, communicate(): pl.pallas_call(comm_kernel, out_shape=(jax.ShapeDtypeStruct((rows, cols),...  129 us
    pallas_call x1, Pallas kernels, finish(): pl.pallas_call(functools.partial(finish_kernel, coef), out_shape=(jax.Sha...  9.06 us

profile of v2, /device:TPU:1, one launch (start us, length us, event | category | flops | bytes accessed | tf_op | source)
XLA Modules:
  0.0 138.5 jit_solution(4419463125661629988)
XLA Ops:
  0.6 128.8 %communicate.1 = (f32[256,5120]{1,0:T(8,128)}, f32[320,8,128]{2,1,0:T(8,128)}, f32[64,64]{1,0:T(8,128)}, f32[64,256]{1,0:T(8,128)}) custom-call(bf16[3072,256]{1,0:T(8,128)(2,1)} %cot.1, bf16[320,3072]{1,0:T(8,128)(2,1)} %bitcast.7, s32[8]{0:T(128)} %lengths.1, f32[256,5120]{1,0:T(8,128)} %bitcast.6, f32[64,5120]{1,0:T(8,128)} %bitcast.8), custom_call_target="tpu_custom_call" | custom-call | tf_op jit(solution)/shard_map/communicate/pallas_call | solution.py:472
  129.4 9.1 %finish.1 = (bf16[256,5120]{1,0:T(8,128)(2,1)}, f32[256,5120]{1,0:T(8,128)}, f32[64,5120]{1,0:T(8,128)}) custom-call(f32[40,64,128]{2,1,0:T(8,128)} %bitcast.9, f32[64,64]{1,0:T(8,128)} %get-tuple-element.11.linv, f32[64,256]{1,0:T(8,128)} %get-tuple-element.12.left_t, f32[256,5120]{1,0:T(8,128)} %get-tuple-element.13.both, bf16[256,5120]{1,0:T(8,128)(2,1)} %weight.1), custom_call_target="tpu_custom_call" | custom-call | tf_op jit(solution)/shard_map/finish/pallas_call | solution.py:588

commit v3 on v2

--- a/solution.py
+++ b/solution.py
@@ -87,18 +87,24 @@
             return {"dp": k * 2 + c}
         if axis == "x":
             return {"tensor": k * 4 + z}
-        return {"tensor": x * 4 + k}
-
-    zl, zr, zo = around(z, 3), around(z, 1), around(z, 2)
-    xl, xr, xo = around(x, 3), around(x, 1), around(x, 2)
+        if axis == "z":
+            return {"tensor": x * 4 + k}
+        if axis == "a":
+            return {"tensor": (1 - c) * (x * 4 + k) + c * (k * 4 + z)}
+        return {"tensor": (1 - c) * (k * 4 + z) + c * (x * 4 + k)}
+
+    pa = (1 - c) * z + c * x
+    pb = (1 - c) * x + c * z
+    al, ar, ao = around(pa, 3), around(pa, 1), around(pa, 2)
+    bl, br, bo = around(pb, 3), around(pb, 1), around(pb, 2)
     tok, rows = cot.shape
     feats = bt.shape[0]
     ha, hb = tok // 2, feats // 2
     mate = along("core", 1 - c)
 
     locals_ = [
-        pltpu.make_async_copy(cot, A.at[z], sl.at[0]),
-        pltpu.make_async_copy(bt, B.at[x], sl.at[1]),
+        pltpu.make_async_copy(cot, A.at[pa], sl.at[0]),
+        pltpu.make_async_copy(bt, B.at[pb], sl.at[1]),
         pltpu.make_async_copy(mom, both, sl.at[2]),
         pltpu.make_async_copy(rft, rfv, sl.at[3]),
     ]
@@ -113,27 +119,27 @@
     sent = []
     for half, right in ((0, True), (1, False), (1, True), (0, False)):
         k = half + (0 if right else 2)
-        ca = remote(cot.at[part_a(half)], A.at[z, part_a(half)], sa.at[k], ra.at[k], along("z", zr if right else zl))
+        ca = remote(cot.at[part_a(half)], A.at[pa, part_a(half)], sa.at[k], ra.at[k], along("a", ar if right else al))
         ca.start()
-        cb = remote(bt.at[part_b(half)], B.at[x, part_b(half)], sb.at[k], rb.at[k], along("x", xr if right else xl))
+        cb = remote(bt.at[part_b(half)], B.at[pb, part_b(half)], sb.at[k], rb.at[k], along("b", br if right else bl))
         cb.start()
         sent += [ca, cb]
     for copy in locals_:
         copy.start()
 
     def got_a(k):
-        remote(A.at[z, part_a(0)], A.at[z, part_a(0)], sa.at[0], ra.at[k], along("z", zr)).wait_recv()
+        remote(A.at[pa, part_a(0)], A.at[pa, part_a(0)], sa.at[0], ra.at[k], along("a", ar)).wait_recv()
 
     def got_b(k):
-        remote(B.at[x, part_b(0)], B.at[x, part_b(0)], sb.at[0], rb.at[k], along("x", xr)).wait_recv()
+        remote(B.at[pb, part_b(0)], B.at[pb, part_b(0)], sb.at[0], rb.at[k], along("b", br)).wait_recv()
 
     def pass_a(k, half, origin, to):
-        copy = remote(A.at[origin, part_a(half)], A.at[origin, part_a(half)], sa.at[k], ra.at[k], along("z", to))
+        copy = remote(A.at[origin, part_a(half)], A.at[origin, part_a(half)], sa.at[k], ra.at[k], along("a", to))
         copy.start()
         sent.append(copy)
 
     def pass_b(k, half, origin, to):
-        copy = remote(B.at[origin, part_b(half)], B.at[origin, part_b(half)], sb.at[k], rb.at[k], along("x", to))
+        copy = remote(B.at[origin, part_b(half)], B.at[origin, part_b(half)], sb.at[k], rb.at[k], along("b", to))
         copy.start()
         sent.append(copy)
 
@@ -167,28 +173,28 @@
         unit(xx, zz, codes.at[xx, zz], scales.at[xx, zz])
 
     def home(xx, zz):
-        remote(codes.at[xx, zz], R.at[xx, z], sc.at[xx, zz], rc.at[xx, z], along("z", zz)).start()
-        remote(scales.at[xx, zz], RS.at[xx, z], ss.at[xx, zz], rs.at[xx, z], along("z", zz)).start()
+        remote(codes.at[xx, zz], R.at[xx, pa], sc.at[xx, zz], rc.at[xx, pa], along("a", zz)).start()
+        remote(scales.at[xx, zz], RS.at[xx, pa], ss.at[xx, zz], rs.at[xx, pa], along("a", zz)).start()
 
     def half_way(xx, side, n):
-        to = along("z", around(z, jnp.where(side == 0, 1, 3)))
-        remote(codes.at[xx, zo], relay.at[side, n], sc.at[xx, zo], rf.at[side, n], to).start()
-        remote(scales.at[xx, zo], relay_s.at[side, n], ss.at[xx, zo], rfs.at[side, n], to).start()
+        to = along("a", around(pa, jnp.where(side == 0, 1, 3)))
+        remote(codes.at[xx, ao], relay.at[side, n], sc.at[xx, ao], rf.at[side, n], to).start()
+        remote(scales.at[xx, ao], relay_s.at[side, n], ss.at[xx, ao], rfs.at[side, n], to).start()
 
     def hand_on(o, wait_only=False):
         side, n = o % 2, o // 2
-        xx = (x, xl, xr, xo)[o]
-        origin, to = (zl, zr) if side == 0 else (zr, zl)
-        one = remote(relay.at[side, n], R.at[xx, origin], sf.at[side, n], rf.at[side, n], along("z", to))
+        xx = (pb, bl, br, bo)[o]
+        origin, to = (al, ar) if side == 0 else (ar, al)
+        one = remote(relay.at[side, n], R.at[xx, origin], sf.at[side, n], rf.at[side, n], along("a", to))
         one.wait_recv()
-        two = remote(relay_s.at[side, n], RS.at[xx, origin], sfs.at[side, n], rfs.at[side, n], along("z", to))
+        two = remote(relay_s.at[side, n], RS.at[xx, origin], sfs.at[side, n], rfs.at[side, n], along("a", to))
         two.wait_recv()
-        remote(relay.at[side, n], R.at[xx, origin], sf.at[side, n], rc.at[xx, origin], along("z", to)).start()
-        remote(relay_s.at[side, n], RS.at[xx, origin], sfs.at[side, n], rs.at[xx, origin], along("z", to)).start()
+        remote(relay.at[side, n], R.at[xx, origin], sf.at[side, n], rc.at[xx, origin], along("a", to)).start()
+        remote(relay_s.at[side, n], RS.at[xx, origin], sfs.at[side, n], rs.at[xx, origin], along("a", to)).start()
 
     locals_[0].wait()
     locals_[1].wait()
-    unit(x, z, R.at[x, z], RS.at[x, z])
+    unit(pb, pa, R.at[pb, pa], RS.at[pb, pa])
     locals_[2].wait()
     locals_[3].wait()
     rank = rft.shape[0]
@@ -207,20 +213,20 @@
     lax.fori_loop(0, both.shape[1] // 256, mom_left, 0)
 
     got_a(0)
-    pass_a(4, 0, zl, zr)
+    pass_a(4, 0, al, ar)
     got_a(3)
-    pass_a(5, 1, zr, zl)
+    pass_a(5, 1, ar, al)
     got_b(0)
-    pass_b(4, 0, xl, xr)
+    pass_b(4, 0, bl, br)
     got_b(3)
-    pass_b(5, 1, xr, xl)
+    pass_b(5, 1, br, bl)
     got_a(1)
     got_a(2)
 
     def own_cols(i, carry):
-        zz = around(z, 3 - 2 * i)
-        made(x, zz)
-        home(x, zz)
+        zz = around(pa, 3 - 2 * i)
+        made(pb, zz)
+        home(pb, zz)
         return carry
 
     lax.fori_loop(0, 2, own_cols, 0)
@@ -228,16 +234,16 @@
     got_b(2)
 
     def next_cols(i, carry):
-        xx = around(x, 3 - 2 * lax.div(i, 3))
+        xx = around(pb, 3 - 2 * lax.div(i, 3))
         m = lax.rem(i, 3)
 
         @pl.when(m == 2)
         def _():
-            unit(xx, z, R.at[xx, z], RS.at[xx, z])
+            unit(xx, pa, R.at[xx, pa], RS.at[xx, pa])
 
         @pl.when(m != 2)
         def _():
-            made(xx, around(z, 3 - 2 * m))
+            made(xx, around(pa, 3 - 2 * m))
 
         return carry
 
@@ -246,15 +252,15 @@
     got_a(5)
 
     def far_rows(i, carry):
-        xx = around(x, jnp.where(i == 0, 0, 5 - 2 * i))
-        made(xx, zo)
+        xx = around(pb, jnp.where(i == 0, 0, 5 - 2 * i))
+        made(xx, ao)
         half_way(xx, lax.rem(i, 2), lax.div(i, 2))
         return carry
 
     lax.fori_loop(0, 3, far_rows, 0)
-    for xx in (xl, xr):
-        home(xx, zl)
-        home(xx, zr)
+    for xx in (bl, br):
+        home(xx, al)
+        home(xx, ar)
     for o in range(3):
         hand_on(o)
     got_b(4)
@@ -263,43 +269,50 @@
     def far_cols(i, carry):
         @pl.when(i == 0)
         def _():
-            made(xo, zo)
-            half_way(xo, 1, 1)
+            made(bo, ao)
+            half_way(bo, 1, 1)
 
         @pl.when(jnp.logical_and(i != 0, i != 3))
         def _():
-            zz = around(z, 5 - 2 * i)
-            made(xo, zz)
-            home(xo, zz)
+            zz = around(pa, 5 - 2 * i)
+            made(bo, zz)
+            home(bo, zz)
 
         @pl.when(i == 3)
         def _():
-            unit(xo, z, R.at[xo, z], RS.at[xo, z])
+            unit(bo, pa, R.at[bo, pa], RS.at[bo, pa])
 
         return carry
 
     lax.fori_loop(0, 4, far_cols, 0)
     hand_on(3)
 
-    def gather_home(o, carry):
-        xx = around(x, jnp.where(o == 0, 0, jnp.where(o == 3, 2, 5 - 2 * o)))
-        for by in (1, 3, 2):
-            zz = around(z, by)
-            remote(codes.at[0, 0], R.at[xx, zz], sc.at[0, 0], rc.at[xx, zz], along("z", zz)).wait_recv()
-            remote(scales.at[0, 0], RS.at[xx, zz], ss.at[0, 0], rs.at[xx, zz], along("z", zz)).wait_recv()
-        for h in range(2):
-            base = xx * (4 * feats) + h * (2 * feats)
-            for i in range(2):
-                S[i * feats : (i + 1) * feats] = R[xx, 2 * h + i].astype(jnp.int32).astype(f32) * RS[xx, 2 * h + i, 0:1]
-            high, low = split(S[...])
-            r = cols_of(base, 2 * feats)
-            v = dot(R2[:, r], high)
-            LT[...] += v[0:rank] + v[rank:] + dot(R2[0:rank, r], low)
-            for i in range(2 * feats // 128):
-                both[:, cols_of(base + 128 * i, 128)] += S[128 * i : 128 * (i + 1)].T
-        return carry
-
-    lax.fori_loop(0, 4, gather_home, 0)
+    late = lax.div(bo, 2)
+
+    def gather_home(n, carry):
+        o, h = lax.div(n, 2), lax.rem(n, 2)
+        xx = around(pb, jnp.where(o == 0, 0, jnp.where(o == 3, 2, 5 - 2 * o)))
+        group = jnp.where(n < 4, 1 - late, late)
+        base = jnp.where(c == 0, xx * 2 + h, lax.rem(n, 4) * 2 + group) * (2 * feats)
+        for i in range(2):
+            xi = jnp.where(c == 0, xx, 2 * group + i)
+            zi = jnp.where(c == 0, 2 * h + i, lax.rem(n, 4))
+
+            @pl.when(zi != pa)
+            def _():
+                remote(codes.at[0, 0], R.at[xi, zi], sc.at[0, 0], rc.at[xi, zi], along("a", ar)).wait_recv()
+                remote(scales.at[0, 0], RS.at[xi, zi], ss.at[0, 0], rs.at[xi, zi], along("a", ar)).wait_recv()
+
+            S[i * feats : (i + 1) * feats] = R[xi, zi].astype(jnp.int32).astype(f32) * RS[xi, zi, 0:1]
+        high, low = split(S[...])
+        r = cols_of(base, 2 * feats)
+        v = dot(R2[:, r], high)
+        LT[...] += v[0:rank] + v[rank:] + dot(R2[0:rank, r], low)
+        for i in range(2 * feats // 128):
+            both[:, cols_of(base + 128 * i, 128)] += S[128 * i : 128 * (i + 1)].T
+        return carry
+
+    lax.fori_loop(0, 8, gather_home, 0)
 
     save = pltpu.make_async_copy(both, both_out, sl.at[4])
     save.start()
@@ -452,13 +465,13 @@
         copy.wait_send()
     for by in (1, 2, 3):
         for xx in range(4):
-            zz = around(z, by)
-            remote(codes.at[xx, zz], R.at[0, 0], sc.at[xx, zz], rc.at[0, 0], along("z", zr)).wait_send()
-            remote(scales.at[xx, zz], RS.at[0, 0], ss.at[xx, zz], rs.at[0, 0], along("z", zr)).wait_send()
+            zz = around(pa, by)
+            remote(codes.at[xx, zz], R.at[0, 0], sc.at[xx, zz], rc.at[0, 0], along("a", ar)).wait_send()
+            remote(scales.at[xx, zz], RS.at[0, 0], ss.at[xx, zz], rs.at[0, 0], along("a", ar)).wait_send()
     for o in range(4):
         side, n = o % 2, o // 2
-        remote(relay.at[side, n], R.at[0, 0], sf.at[side, n], rc.at[0, 0], along("z", zr)).wait_send()
-        remote(relay_s.at[side, n], RS.at[0, 0], sfs.at[side, n], rs.at[0, 0], along("z", zr)).wait_send()
+        remote(relay.at[side, n], R.at[0, 0], sf.at[side, n], rc.at[0, 0], along("a", ar)).wait_send()
+        remote(relay_s.at[side, n], RS.at[0, 0], sfs.at[side, n], rs.at[0, 0], along("a", ar)).wait_send()
     save.wait()
 
 

time: 139 us -> 133 us (0.957)
  Pallas kernels: 138 us -> 132 us
    pallas_call x1, Pallas kernels: 129 us -> 123 us  [communicate(): pl.pallas_call(comm_kernel, out_shape=(jax.ShapeDtypeStruct((rows, cols),...]
where the time goes in v3:
time: 133 us
  Pallas kernels  132 us (99%)
    pallas_call x1, Pallas kernels, communicate(): pl.pallas_call(comm_kernel, out_shape=(jax.ShapeDtypeStruct((rows, cols),...  123 us
    pallas_call x1, Pallas kernels, finish(): pl.pallas_call(functools.partial(finish_kernel, coef), out_shape=(jax.Sha...  9.07 us

profile of v3, /device:TPU:1, one launch (start us, length us, event | category | flops | bytes accessed | tf_op | source)
XLA Modules:
  0.0 132.9 jit_solution(12315781447628952955)
XLA Ops:
  0.6 123.1 %communicate.1 = (f32[256,5120]{1,0:T(8,128)}, f32[320,8,128]{2,1,0:T(8,128)}, f32[64,64]{1,0:T(8,128)}, f32[64,256]{1,0:T(8,128)}) custom-call(bf16[3072,256]{1,0:T(8,128)(2,1)} %cot.1, bf16[320,3072]{1,0:T(8,128)(2,1)} %bitcast.7, s32[8]{0:T(128)} %lengths.1, f32[256,5120]{1,0:T(8,128)} %bitcast.6, f32[64,5120]{1,0:T(8,128)} %bitcast.8), custom_call_target="tpu_custom_call" | custom-call | tf_op jit(solution)/shard_map/communicate/pallas_call | solution.py:485
  123.8 9.1 %finish.1 = (bf16[256,5120]{1,0:T(8,128)(2,1)}, f32[256,5120]{1,0:T(8,128)}, f32[64,5120]{1,0:T(8,128)}) custom-call(f32[40,64,128]{2,1,0:T(8,128)} %bitcast.9, f32[64,64]{1,0:T(8,128)} %get-tuple-element.11.linv, f32[64,256]{1,0:T(8,128)} %get-tuple-element.12.left_t, f32[256,5120]{1,0:T(8,128)} %get-tuple-element.13.both, bf16[256,5120]{1,0:T(8,128)(2,1)} %weight.1), custom_call_target="tpu_custom_call" | custom-call | tf_op jit(solution)/shard_map/finish/pallas_call | solution.py:601

commit v4 on v3

--- a/solution.py
+++ b/solution.py
@@ -18,6 +18,8 @@
 VMEM = pltpu.VMEM
 DMA = pltpu.SemaphoreType.DMA
 CODES = 32767.0
+COMM_BYTES = 38 * 2**20
+FINISH_BYTES = 16 * 2**20
 DEPTH = 768
 
 
@@ -25,8 +27,8 @@
     return pl.BlockSpec(memory_space=pltpu.VMEM)
 
 
-def anyspec():
-    return pl.BlockSpec(memory_space=pl.ANY)
+def hspec():
+    return pl.BlockSpec(memory_space=pltpu.HBM)
 
 
 def sspec():
@@ -68,10 +70,19 @@
     pl.semaphore_wait(barrier, len(peers))
 
 
+def parts_of(tiles):
+    most = tiles // 16 - 2 * (tiles // 48)
+    return (most * 16, tiles // 48 * 16, tiles // 48 * 16)
+
+
+def tile_column(tiles, j):
+    return tiles[pl.ds(j * 8, 8)].reshape(64, 128)
+
+
 def comm_kernel(
-    cot, bt, lengths, mom, rft, both_out, out, linv_out, left_out,
-    A, B, codes, scales, R, RS, relay, relay_s, acc, keep, S, R2, both, rfv,
-    LT, L0, L1, LL, T, D, P1, P2, P3, G1, G2, M,
+    cot, bt, lengths, mom, rft, both, RT, norm_out, ortho_out,
+    A, B, codes, scales, R, RS, relay, relay_s, acc, keep, S, R2, rfv,
+    LT, L0, L1, LL, LV, T, D, out, P1, P2, P3, G1, G2, M,
     sl, sa, ra, sb, rb, sc, ss, rc, rs, sf, sfs, rf, rfs, send, recv,
 ):
     t = lax.axis_index("tensor")
@@ -314,8 +325,6 @@
 
     lax.fori_loop(0, 8, gather_home, 0)
 
-    save = pltpu.make_async_copy(both, both_out, sl.at[4])
-    save.start()
     pending = []
 
     def swap(stage, src, dst):
@@ -344,7 +353,6 @@
     L1[y] = LT[...] + L0[...]
     spread(1, "y", lambda k: L1.at[y], lambda k: L1.at[k])()
     left = (L1[0] + L1[1] + L1[2] + L1[3]) * (1.0 / 8.0)
-    left_out[...] = left
     left_high, left_low = split(left)
     LL[0:rank] = left_high
     LL[rank : 2 * rank] = left_low
@@ -377,31 +385,34 @@
 
     lax.fori_loop(0, half // 20, add_core, 0)
 
-    n1, n2 = half // 8, half // 32
-    orders = (("y", "x", "z"), ("x", "z", "y"))
-    base = [mine + k * (half // 2) for k in range(2)]
+    orders = (("y", "x", "z"), ("x", "z", "y"), ("z", "y", "x"))
+    sizes = parts_of(half)
+    base = [mine, mine + sizes[0], mine + sizes[0] + sizes[1]]
+    n1 = [size // 4 for size in sizes]
+    n2 = [size // 16 for size in sizes]
     zeroth, first, second, third, fourth = [], [], [], [], []
     for k, (a1, a2, a3) in enumerate(orders):
         zeroth.append(
             spread(
                 4 + k, a1,
-                lambda q, k=k: T.at[pl.ds(base[k] + q * n1, n1)],
-                lambda q, k=k: P1.at[k, q],
+                lambda q, k=k: T.at[pl.ds(base[k] + q * n1[k], n1[k])],
+                lambda q, k=k: P1.at[k, q, 0 : n1[k]],
             )
         )
     gram_wait()
     G2[x] = G1[0] + G1[1] + G1[2] + G1[3]
-    gram_wait = spread(8, "x", lambda k: G2.at[x], lambda k: G2.at[k])
+    gram_wait = spread(19, "x", lambda k: G2.at[x], lambda k: G2.at[k])
     for k, (a1, a2, a3) in enumerate(orders):
         me = place[a1]
-        P1[k, me] = T[pl.ds(base[k] + me * n1, n1)]
+        P1[k, me, 0 : n1[k]] = T[pl.ds(base[k] + me * n1[k], n1[k])]
         zeroth[k]()
-        P1[k, 0] = P1[k, 0] + P1[k, 1] + P1[k, 2] + P1[k, 3]
+        low = slice(0, n1[k])
+        P1[k, 0, low] = P1[k, 0, low] + P1[k, 1, low] + P1[k, 2, low] + P1[k, 3, low]
         first.append(
             spread(
-                6 + k, a2,
-                lambda q, k=k: P1.at[k, 0, pl.ds(q * n2, n2)],
-                lambda q, k=k: P2.at[k, q],
+                7 + k, a2,
+                lambda q, k=k: P1.at[k, 0, pl.ds(q * n2[k], n2[k])],
+                lambda q, k=k: P2.at[k, q, 0 : n2[k]],
             )
         )
     row_id = lax.broadcasted_iota(jnp.int32, (rank, 2 * rank), 0)
@@ -423,43 +434,67 @@
     lax.fori_loop(cuts[0], cuts[1], pivot, 0)
     for k, (a1, a2, a3) in enumerate(orders):
         me = place[a2]
-        P2[k, me] = P1[k, 0, pl.ds(me * n2, n2)]
+        low = slice(0, n2[k])
+        P2[k, me, low] = P1[k, 0, pl.ds(me * n2[k], n2[k])]
         first[k]()
         m3 = place[a3]
-        P3[k, m3] = P2[k, 0] + P2[k, 1] + P2[k, 2] + P2[k, 3]
-        second.append(spread(9 + k, a3, lambda q, k=k, m3=m3: P3.at[k, m3], lambda q, k=k: P3.at[k, q]))
+        P3[k, m3, low] = P2[k, 0, low] + P2[k, 1, low] + P2[k, 2, low] + P2[k, 3, low]
+        second.append(
+            spread(
+                10 + k, a3,
+                lambda q, k=k, m3=m3: P3.at[k, m3, 0 : n2[k]],
+                lambda q, k=k: P3.at[k, q, 0 : n2[k]],
+            )
+        )
     lax.fori_loop(cuts[1], cuts[2], pivot, 0)
     for k, (a1, a2, a3) in enumerate(orders):
         second[k]()
-        row = base[k] + place[a1] * n1
-        spot = row + place[a2] * n2
-        out[pl.ds(spot, n2)] = P3[k, 0] + P3[k, 1] + P3[k, 2] + P3[k, 3]
+        row = base[k] + place[a1] * n1[k]
+        spot = row + place[a2] * n2[k]
+        low = slice(0, n2[k])
+        out[pl.ds(spot, n2[k])] = P3[k, 0, low] + P3[k, 1, low] + P3[k, 2, low] + P3[k, 3, low]
         third.append(
             spread(
-                11 + k, a2,
-                lambda q, spot=spot: out.at[pl.ds(spot, n2)],
-                lambda q, row=row: out.at[pl.ds(row + q * n2, n2)],
+                13 + k, a2,
+                lambda q, spot=spot, k=k: out.at[pl.ds(spot, n2[k])],
+                lambda q, row=row, k=k: out.at[pl.ds(row + q * n2[k], n2[k])],
             )
         )
     lax.fori_loop(cuts[2], cuts[3], pivot, 0)
     for k, (a1, a2, a3) in enumerate(orders):
         third[k]()
-        row = base[k] + place[a1] * n1
+        row = base[k] + place[a1] * n1[k]
         fourth.append(
             spread(
-                13 + k, a1,
-                lambda q, row=row: out.at[pl.ds(row, n1)],
-                lambda q, k=k: out.at[pl.ds(base[k] + q * n1, n1)],
+                16 + k, a1,
+                lambda q, row=row, k=k: out.at[pl.ds(row, n1[k])],
+                lambda q, k=k: out.at[pl.ds(base[k] + q * n1[k], n1[k])],
             )
         )
     lax.fori_loop(cuts[3], cuts[4], pivot, 0)
     m = M[...]
     diag = jnp.sum(jnp.where(lane_id == row_id, m, 0.0), axis=1, keepdims=True)
-    linv_out[...] = pltpu.roll(m / jnp.sqrt(diag), rank, 1)[:, 0:rank]
-    fourth[0]()
-    fourth[1]()
-    swap(15, out.at[pl.ds(mine, half)], out.at[pl.ds(mine, half)])
-    remote(out.at[pl.ds(theirs, half)], out.at[pl.ds(theirs, half)], send.at[15, 0], recv.at[15, 0], mate).wait_recv()
+    linv = pltpu.roll(m / jnp.sqrt(diag), rank, 1)[:, 0:rank]
+    ortho_out[...] = jnp.dot(linv, (L1[0] + L1[1] + L1[2] + L1[3]) * (1.0 / 8.0), precision=HI, preferred_element_type=f32)
+    v_high, v_low = split(linv * (1.0 / 8.0))
+    LV[0] = v_high
+    LV[1] = v_low
+    for k in range(3):
+        fourth[k]()
+    swap(20, out.at[pl.ds(mine, half)], out.at[pl.ds(mine, half)])
+
+    def right(j, sq):
+        high, low = split(jnp.concatenate([tile_column(out, 2 * j), tile_column(out, 2 * j + 1)], axis=1))
+        v = dot(LV[0], high) + dot(LV[1], high) + dot(LV[0], low)
+        RT[:, cols_of(j * 256, 256)] = v
+        return sq + v * v
+
+    sq = lax.fori_loop(blocks * c, blocks * (1 + c), right, jnp.zeros((rank, 256), f32))
+    remote(out.at[pl.ds(theirs, half)], out.at[pl.ds(theirs, half)], send.at[20, 0], recv.at[20, 0], mate).wait_recv()
+    sq_other = lax.fori_loop(blocks * (1 - c), blocks * (2 - c), right, jnp.zeros((rank, 256), f32))
+    total = jnp.where(c == 0, sq, sq_other) + jnp.where(c == 0, sq_other, sq)
+    norm = lax.rsqrt(jnp.sum(total, axis=1, keepdims=True) + EPS)
+    norm_out[...] = jnp.broadcast_to(norm, norm_out.shape)
 
     for copy in pending + sent:
         copy.wait_send()
@@ -472,7 +507,6 @@
         side, n = o % 2, o // 2
         remote(relay.at[side, n], R.at[0, 0], sf.at[side, n], rc.at[0, 0], along("a", ar)).wait_send()
         remote(relay_s.at[side, n], RS.at[0, 0], sfs.at[side, n], rs.at[0, 0], along("a", ar)).wait_send()
-    save.wait()
 
 
 def communicate(cot, bt, lengths, mom, rft):
@@ -481,17 +515,18 @@
     rank, cols = rft.shape
     tiles = cols // 128 * (rank // 8)
     half = tiles // 2
-    n1, n2 = half // 8, half // 32
+    most = max(parts_of(half))
+    n1, n2 = most // 4, most // 16
     return pl.pallas_call(
         comm_kernel,
         out_shape=(
             jax.ShapeDtypeStruct((rows, cols), f32),
-            jax.ShapeDtypeStruct((tiles, 8, 128), f32),
-            jax.ShapeDtypeStruct((rank, rank), f32),
+            jax.ShapeDtypeStruct((rank, cols), f32),
+            jax.ShapeDtypeStruct((rank, 128), f32),
             jax.ShapeDtypeStruct((rank, rows), f32),
         ),
-        in_specs=[anyspec(), anyspec(), sspec(), anyspec(), anyspec()],
-        out_specs=(anyspec(), vspec(), vspec(), vspec()),
+        in_specs=[hspec(), hspec(), sspec(), hspec(), hspec()],
+        out_specs=(vspec(), vspec(), vspec(), vspec()),
         scratch_shapes=[
             VMEM((4, tok, rows), bf16),
             VMEM((4, feats, tok), bf16),
@@ -505,85 +540,60 @@
             VMEM((16, tok), bf16),
             VMEM((2 * feats, rows), f32),
             VMEM((2 * rank, cols), bf16),
-            VMEM((rows, cols), f32),
             VMEM((rank, cols), f32),
             VMEM((rank, rows), f32),
             VMEM((rank, rows), f32),
             VMEM((4, rank, rows), f32),
             VMEM((2 * rank, rows), bf16),
+            VMEM((2, rank, rank), bf16),
             VMEM((tiles, 8, 128), f32),
             VMEM((half, 8, 128), f32),
-            VMEM((2, 4, n1, 8, 128), f32),
-            VMEM((2, 4, n2, 8, 128), f32),
-            VMEM((2, 4, n2, 8, 128), f32),
+            VMEM((tiles, 8, 128), f32),
+            VMEM((3, 4, n1, 8, 128), f32),
+            VMEM((3, 4, n2, 8, 128), f32),
+            VMEM((3, 4, n2, 8, 128), f32),
             VMEM((4, rank, rank), f32),
             VMEM((4, rank, rank), f32),
             VMEM((rank, 2 * rank), f32),
             DMA((5,)), DMA((6,)), DMA((6,)), DMA((6,)), DMA((6,)),
             DMA((4, 4)), DMA((4, 4)), DMA((4, 4)), DMA((4, 4)),
             DMA((2, 2)), DMA((2, 2)), DMA((2, 2)), DMA((2, 2)),
-            DMA((16, 4)), DMA((16, 4)),
+            DMA((21, 4)), DMA((21, 4)),
         ],
-        compiler_params=pltpu.CompilerParams(collective_id=0, has_side_effects=True),
+        compiler_params=pltpu.CompilerParams(
+            collective_id=0, has_side_effects=True, vmem_limit_bytes=COMM_BYTES
+        ),
         name="communicate",
     )(cot, bt, lengths, mom, rft)
 
 
 def finish_kernel(
-    coef, total, linv, left_t, both, weight, new_weight, new_mom, new_right_t,
-    bv, wv, RT, R3, O3, NR, isem, osem,
+    coef, right_t, norm, ortho_t, both, weight, new_weight, new_mom, new_right_t,
+    bv, wv, NR, O3, osem,
 ):
     rows, cols = both.shape
-    rank = linv.shape[0]
     wide = cols // 8
-
-    def fetch(i):
-        r = cols_of(i * wide, wide)
-        return (
-            pltpu.make_async_copy(both.at[:, r], bv.at[:, r], isem.at[i, 0]),
-            pltpu.make_async_copy(weight.at[:, r], wv.at[:, r], isem.at[i, 1]),
-        )
 
     def store(i):
         r = cols_of(i * wide, wide)
         return (
             pltpu.make_async_copy(bv.at[:, r], new_mom.at[:, r], osem.at[i, 0]),
             pltpu.make_async_copy(wv.at[:, r], new_weight.at[:, r], osem.at[i, 1]),
+            pltpu.make_async_copy(NR.at[:, r], new_right_t.at[:, r], osem.at[i, 2]),
         )
 
-    for i in range(8):
-        for copy in fetch(i):
-            copy.start()
-    l_high, l_low = split(linv[...] * (1.0 / 8.0))
-
-    def col(j, sq):
-        high, low = split(jnp.concatenate([total[2 * j], total[2 * j + 1]], axis=1))
-        v = dot(l_high, high) + dot(l_low, high) + dot(l_high, low)
-        r = cols_of(j * 256, 256)
-        RT[:, r] = v
-        v_high, v_low = split(v)
-        R3[0:rank, r] = v_high
-        R3[rank : 2 * rank, r] = v_low
-        R3[2 * rank : 3 * rank, r] = v_high
-        return sq + v * v
-
-    sq = lax.fori_loop(0, cols // 256, col, jnp.zeros((rank, 256), f32))
-    norm = lax.rsqrt(jnp.sum(sq, axis=1, keepdims=True) + EPS)
-    NR[...] = RT[...] * norm
-    tell = pltpu.make_async_copy(NR, new_right_t, osem.at[8, 0])
-    tell.start()
-    ortho_t = jnp.dot(linv[...], left_t[...], precision=HI, preferred_element_type=f32)
-    both_t = jnp.concatenate([ortho_t * (1.0 - MU), ortho_t * (norm * coef)], axis=1)
+    both_t = jnp.concatenate([ortho_t[...] * (1.0 - MU), ortho_t[...] * (norm[:, 0:1] * coef)], axis=1)
     o_high, o_low = split(both_t)
     O3[...] = jnp.concatenate([o_high, o_high, o_low], axis=0).T
 
     def work(i, carry):
-        for copy in fetch(i):
-            copy.wait()
         r = cols_of(i * wide, wide)
-        low = dot(O3[...], R3[:, r])
-        bv[:, r] = bv[:, r] - low[0:rows]
-        wv[:, r] = (wv[:, r].astype(f32) - low[rows:]).astype(bf16)
+        v = right_t[:, r]
+        high, low = split(v)
+        change = dot(O3[...], jnp.concatenate([high, low, high], axis=0))
+        bv[:, r] = both[:, r] - change[0:rows]
+        wv[:, r] = (weight[:, r].astype(f32) - change[rows:]).astype(bf16)
+        NR[:, r] = v * norm[:, 0:1]
         for copy in store(i):
             copy.start()
         return carry
@@ -592,12 +602,11 @@
     for i in range(8):
         for copy in store(i):
             copy.wait()
-    tell.wait()
-
-
-def finish(coef, total, linv, left_t, both, weight):
+
+
+def finish(coef, right_t, norm, ortho_t, both, weight):
     rows, cols = both.shape
-    rank = linv.shape[0]
+    rank = right_t.shape[0]
     return pl.pallas_call(
         functools.partial(finish_kernel, coef),
         out_shape=(
@@ -605,30 +614,28 @@
             jax.ShapeDtypeStruct((rows, cols), f32),
             jax.ShapeDtypeStruct((rank, cols), f32),
         ),
-        in_specs=[vspec(), vspec(), vspec(), anyspec(), anyspec()],
-        out_specs=(anyspec(), anyspec(), anyspec()),
+        in_specs=[vspec()] * 5,
+        out_specs=(hspec(), hspec(), hspec()),
         scratch_shapes=[
             VMEM((rows, cols), f32),
             VMEM((rows, cols), bf16),
             VMEM((rank, cols), f32),
-            VMEM((3 * rank, cols), bf16),
             VMEM((2 * rows, 3 * rank), bf16),
-            VMEM((rank, cols), f32),
-            DMA((8, 2)),
-            DMA((9, 2)),
+            DMA((8, 3)),
         ],
+        compiler_params=pltpu.CompilerParams(vmem_limit_bytes=FINISH_BYTES),
         name="finish",
-    )(total, linv, left_t, both, weight)
+    )(right_t, norm, ortho_t, both, weight)
 
 
 def per_device(inputs, cotangent, lengths, momentum, weight, right_factor):
-    both, total, linv, left_t = communicate(cotangent, inputs.T, lengths, momentum[0], right_factor.T)
-    rank = linv.shape[0]
+    stay = lambda v: pltpu.with_memory_space_constraint(v, pltpu.HBM)
+    both, right_t, norm, ortho_t = communicate(
+        stay(cotangent), stay(inputs.T), stay(lengths), stay(momentum[0]), stay(right_factor.T)
+    )
     rows_all = both.shape[0] * lax.axis_size("tensor")
     coef = LR * math.sqrt(rows_all / both.shape[1])
-    new_weight, new_mom, new_right_t = finish(
-        coef, total.reshape(-1, rank, 128), linv, left_t, both, weight
-    )
+    new_weight, new_mom, new_right_t = finish(coef, right_t, norm, ortho_t, both, weight)
     return (new_weight, new_mom[None], new_right_t.T)
 
 

time: 133 us -> 128 us (0.962)
  Pallas kernels: 132 us -> 127 us
    pallas_call x1, Pallas kernels: 9.07 us -> 4.21 us  [finish(): pl.pallas_call(functools.partial(finish_kernel, coef), out_shape=(jax.Sha...]
where the time goes in v4:
time: 128 us
  Pallas kernels  127 us (99%)
    pallas_call x1, Pallas kernels, communicate(): pl.pallas_call(comm_kernel, out_shape=(jax.ShapeDtypeStruct((rows, cols),...  123 us
    pallas_call x1, Pallas kernels, finish(): pl.pallas_call(functools.partial(finish_kernel, coef), out_shape=(jax.Sha...  4.21 us

profile of v4, /device:TPU:1, one launch (start us, length us, event | category | flops | bytes accessed | tf_op | source)
XLA Modules:
  0.0 127.9 jit_solution(5336769145307333315)
XLA Ops:
  0.6 0.0 copy-start
  0.6 123.0 %communicate.1 = (f32[256,5120]{1,0:T(8,128)S(1)}, f32[64,5120]{1,0:T(8,128)S(1)}, f32[64,128]{1,0:T(8,128)S(1)}, f32[64,256]{1,0:T(8,128)S(1)}) custom-call(bf16[3072,256]{1,0:T(8,128)(2,1)} %cot.1, bf16[320,3072]{1,0:T(8,128)(2,1)} %bitcast.6, s32[8]{0:T(128)} %lengths.1, f32[256,5120]{1,0:T(8,128)} %bitcast.5, f32[64,5120]{1,0:T(8,128)} %bitcast.7), custom_call_target="tpu_custom_call" | custom-call | tf_op jit(solution)/shard_map/communicate/pallas_call | solution.py:520
  123.6 0.0 copy-done
  123.6 4.2 %finish.1 = (bf16[256,5120]{1,0:T(8,128)(2,1)}, f32[256,5120]{1,0:T(8,128)}, f32[64,5120]{1,0:T(8,128)}) custom-call(f32[64,5120]{1,0:T(8,128)S(1)} %get-tuple-element.10.right_t, f32[64,128]{1,0:T(8,128)S(1)} %get-tuple-element.11.norm, f32[64,256]{1,0:T(8,128)S(1)} %get-tuple-element.12.ortho_t, f32[256,5120]{1,0:T(8,128)S(1)} %get-tuple-element.13.both, ...), custom_call_target="tpu_custom_call" | custom-call | tf_op jit(solution)/shard_map/finish/pallas_call | solution.py:610
Async XLA Ops:
  0.6 123.0 %copy-start = (bf16[256,5120]{1,0:T(8,128)(2,1)S(1)}, bf16[256,5120]{1,0:T(8,128)(2,1)}, u32[]{:S(2)}) copy-start(bf16[256,5120]{1,0:T(8,128)(2,1)} %weight.1) | copy-start | bytes 7864324

commit v5 on v4

--- a/solution.py
+++ b/solution.py
@@ -296,18 +296,19 @@
         return carry
 
     lax.fori_loop(0, 4, far_cols, 0)
-    hand_on(3)
-
-    late = lax.div(bo, 2)
+    late, far = lax.div(bo, 2), lax.div(ao, 2)
 
     def gather_home(n, carry):
-        o, h = lax.div(n, 2), lax.rem(n, 2)
+        o = jnp.where(n < 6, lax.rem(n, 3), 3)
+        h = jnp.where(jnp.logical_or(n < 3, n == 6), 1 - far, far)
         xx = around(pb, jnp.where(o == 0, 0, jnp.where(o == 3, 2, 5 - 2 * o)))
         group = jnp.where(n < 4, 1 - late, late)
-        base = jnp.where(c == 0, xx * 2 + h, lax.rem(n, 4) * 2 + group) * (2 * feats)
+        m = lax.rem(n, 4)
+        zz = around(pa, jnp.where(m == 0, 0, jnp.where(m == 3, 2, 5 - 2 * m)))
+        base = jnp.where(c == 0, xx * 2 + h, zz * 2 + group) * (2 * feats)
         for i in range(2):
             xi = jnp.where(c == 0, xx, 2 * group + i)
-            zi = jnp.where(c == 0, 2 * h + i, lax.rem(n, 4))
+            zi = jnp.where(c == 0, 2 * h + i, zz)
 
             @pl.when(zi != pa)
             def _():
@@ -323,12 +324,14 @@
             both[:, cols_of(base + 128 * i, 128)] += S[128 * i : 128 * (i + 1)].T
         return carry
 
-    lax.fori_loop(0, 8, gather_home, 0)
+    lax.fori_loop(0, 3, gather_home, 0)
+    hand_on(3)
+    lax.fori_loop(3, 8, gather_home, 0)
 
     pending = []
 
-    def swap(stage, src, dst):
-        copy = remote(src, dst, send.at[stage, 0], recv.at[stage, 0], mate)
+    def swap(stage, src, dst, k=0):
+        copy = remote(src, dst, send.at[stage, k], recv.at[stage, k], mate)
         copy.start()
         pending.append(copy)
         return copy
@@ -372,26 +375,35 @@
             T[pl.ds(g * 16 + i * 8, 8)] = v[:, 128 * i : 128 * (i + 1)].reshape(8, 8, 128)
         return carry
 
-    lax.fori_loop(blocks * (1 - c), blocks * (2 - c), block, 0)
-    mine, theirs = c * half, (1 - c) * half
-    core_wait = swap(3, T.at[pl.ds(theirs, half)], D)
-    lax.fori_loop(blocks * c, blocks * (1 + c), block, 0)
-    core_wait.wait_recv()
-
-    def add_core(g, carry):
-        r = pl.ds(mine + g * 20, 20)
-        T[r] = T[r] + D[pl.ds(g * 20, 20)]
-        return carry
-
-    lax.fori_loop(0, half // 20, add_core, 0)
-
     orders = (("y", "x", "z"), ("x", "z", "y"), ("z", "y", "x"))
     sizes = parts_of(half)
-    base = [mine, mine + sizes[0], mine + sizes[0] + sizes[1]]
+    begin = (0, sizes[0], sizes[0] + sizes[1])
+    mine, theirs = c * half, (1 - c) * half
+    base = [mine + start for start in begin]
     n1 = [size // 4 for size in sizes]
     n2 = [size // 16 for size in sizes]
+
+    def part_blocks(side, k):
+        start = blocks * side + begin[k] // 16
+        return start, start + sizes[k] // 16
+
+    core_waits = []
+    for k in range(3):
+        lax.fori_loop(*part_blocks(1 - c, k), block, 0)
+        core_waits.append(
+            swap(3, T.at[pl.ds(theirs + begin[k], sizes[k])], D.at[pl.ds(begin[k], sizes[k])], k)
+        )
+
+    def add_core(g, carry):
+        r = pl.ds(mine + g * 16, 16)
+        T[r] = T[r] + D[pl.ds(g * 16, 16)]
+        return carry
+
     zeroth, first, second, third, fourth = [], [], [], [], []
     for k, (a1, a2, a3) in enumerate(orders):
+        lax.fori_loop(*part_blocks(c, k), block, 0)
+        core_waits[k].wait_recv()
+        lax.fori_loop(begin[k] // 16, (begin[k] + sizes[k]) // 16, add_core, 0)
         zeroth.append(
             spread(
                 4 + k, a1,
@@ -481,7 +493,8 @@
     LV[1] = v_low
     for k in range(3):
         fourth[k]()
-    swap(20, out.at[pl.ds(mine, half)], out.at[pl.ds(mine, half)])
+        r = pl.ds(base[k], sizes[k])
+        swap(20, out.at[r], out.at[r], k)
 
     def right(j, sq):
         high, low = split(jnp.concatenate([tile_column(out, 2 * j), tile_column(out, 2 * j + 1)], axis=1))
@@ -489,9 +502,14 @@
         RT[:, cols_of(j * 256, 256)] = v
         return sq + v * v
 
-    sq = lax.fori_loop(blocks * c, blocks * (1 + c), right, jnp.zeros((rank, 256), f32))
-    remote(out.at[pl.ds(theirs, half)], out.at[pl.ds(theirs, half)], send.at[20, 0], recv.at[20, 0], mate).wait_recv()
-    sq_other = lax.fori_loop(blocks * (1 - c), blocks * (2 - c), right, jnp.zeros((rank, 256), f32))
+    sq = jnp.zeros((rank, 256), f32)
+    sq_other = sq
+    for k in range(3):
+        sq = lax.fori_loop(*part_blocks(c, k), right, sq)
+    for k in range(3):
+        r = pl.ds(theirs + begin[k], sizes[k])
+        remote(out.at[r], out.at[r], send.at[20, k], recv.at[20, k], mate).wait_recv()
+        sq_other = lax.fori_loop(*part_blocks(1 - c, k), right, sq_other)
     total = jnp.where(c == 0, sq, sq_other) + jnp.where(c == 0, sq_other, sq)
     norm = lax.rsqrt(jnp.sum(total, axis=1, keepdims=True) + EPS)
     norm_out[...] = jnp.broadcast_to(norm, norm_out.shape)

time: 128 us -> 126 us (0.984)
    pallas_call x1, Pallas kernels: 123 us -> 121 us  [communicate(): pl.pallas_call(comm_kernel, out_shape=(jax.ShapeDtypeStruct((rows, cols),...]
where the time goes in v5:
time: 126 us
  Pallas kernels  126 us (100%)
    pallas_call x1, Pallas kernels, communicate(): pl.pallas_call(comm_kernel, out_shape=(jax.ShapeDtypeStruct((rows, cols),...  121 us
    pallas_call x1, Pallas kernels, finish(): pl.pallas_call(functools.partial(finish_kernel, coef), out_shape=(jax.Sha...  4.2 us

profile of v5, /device:TPU:1, one launch (start us, length us, event | category | flops | bytes accessed | tf_op | source)
XLA Modules:
  0.0 126.3 jit_solution(2217099625148165876)
XLA Ops:
  0.6 0.0 copy-start
  0.6 121.4 %communicate.1 = (f32[256,5120]{1,0:T(8,128)S(1)}, f32[64,5120]{1,0:T(8,128)S(1)}, f32[64,128]{1,0:T(8,128)S(1)}, f32[64,256]{1,0:T(8,128)S(1)}) custom-call(bf16[3072,256]{1,0:T(8,128)(2,1)} %cot.1, bf16[320,3072]{1,0:T(8,128)(2,1)} %bitcast.6, s32[8]{0:T(128)} %lengths.1, f32[256,5120]{1,0:T(8,128)} %bitcast.5, f32[64,5120]{1,0:T(8,128)} %bitcast.7), custom_call_target="tpu_custom_call" | custom-call | tf_op jit(solution)/shard_map/communicate/pallas_call | solution.py:538
  122.1 0.0 copy-done
  122.1 4.2 %finish.1 = (bf16[256,5120]{1,0:T(8,128)(2,1)}, f32[256,5120]{1,0:T(8,128)}, f32[64,5120]{1,0:T(8,128)}) custom-call(f32[64,5120]{1,0:T(8,128)S(1)} %get-tuple-element.10.right_t, f32[64,128]{1,0:T(8,128)S(1)} %get-tuple-element.11.norm, f32[64,256]{1,0:T(8,128)S(1)} %get-tuple-element.12.ortho_t, f32[256,5120]{1,0:T(8,128)S(1)} %get-tuple-element.13.both, ...), custom_call_target="tpu_custom_call" | custom-call | tf_op jit(solution)/shard_map/finish/pallas_call | solution.py:628
Async XLA Ops:
  0.6 121.4 %copy-start = (bf16[256,5120]{1,0:T(8,128)(2,1)S(1)}, bf16[256,5120]{1,0:T(8,128)(2,1)}, u32[]{:S(2)}) copy-start(bf16[256,5120]{1,0:T(8,128)(2,1)} %weight.1) | copy-start | bytes 7864324

commit v6 on v5

--- a/solution.py
+++ b/solution.py
@@ -82,7 +82,7 @@
 def comm_kernel(
     cot, bt, lengths, mom, rft, both, RT, norm_out, ortho_out,
     A, B, codes, scales, R, RS, relay, relay_s, acc, keep, S, R2, rfv,
-    LT, L0, L1, LL, LV, T, D, out, P1, P2, P3, G1, G2, M,
+    LT, L0, L1, LF, LL, LV, T, D, out, P1, P2, P3, G1, G2, M,
     sl, sa, ra, sb, rb, sc, ss, rc, rs, sf, sfs, rf, rfs, send, recv,
 ):
     t = lax.axis_index("tensor")
@@ -338,30 +338,34 @@
 
     def spread(stage, axis, src, dst):
         me = place[axis]
-        waits = []
+        waits = {}
         for q in (2, 1, 3):
             k = around(me, q)
             copy = remote(src(k), dst(me), send.at[stage, q], recv.at[stage, q], along(axis, k))
             copy.start()
             pending.append(copy)
-            waits.append(remote(src(k), dst(around(me, 4 - q)), send.at[stage, q], recv.at[stage, q], along(axis, k)))
-
-        def wait():
-            for w in waits:
-                w.wait_recv()
+            waits[q] = remote(src(k), dst(around(me, 4 - q)), send.at[stage, q], recv.at[stage, q], along(axis, k))
+
+        def wait(which=(2, 1, 3)):
+            for q in which:
+                waits[q].wait_recv()
 
         return wait
 
-    swap(0, LT, L0).wait_recv()
-    L1[y] = LT[...] + L0[...]
+    here, there = pl.ds(c * (rank // 2), rank // 2), pl.ds((1 - c) * (rank // 2), rank // 2)
+    swap(0, LT.at[there], L0).wait_recv()
+    L1[y] = LT[here] + L0[...]
     spread(1, "y", lambda k: L1.at[y], lambda k: L1.at[k])()
-    left = (L1[0] + L1[1] + L1[2] + L1[3]) * (1.0 / 8.0)
+    LF[here] = (L1[0] + L1[1] + L1[2] + L1[3]) * (1.0 / 8.0)
+    swap(2, LF.at[here], LF.at[here])
+    remote(LF.at[there], LF.at[there], send.at[2, 0], recv.at[2, 0], mate).wait_recv()
+    left = LF[...]
     left_high, left_low = split(left)
     LL[0:rank] = left_high
     LL[rank : 2 * rank] = left_low
     v = dot(LL[...], left_high, ((1,), (1,)))
     G1[z] = v[0:rank] + v[rank:] + dot(left_high, left_low, ((1,), (1,)))
-    gram_wait = spread(2, "z", lambda k: G1.at[z], lambda k: G1.at[k])
+    gram_wait = spread(21, "z", lambda k: G1.at[z], lambda k: G1.at[k])
 
     tiles = both.shape[1] // 128 * (rank // 8)
     half = tiles // 2
@@ -399,7 +403,7 @@
         T[r] = T[r] + D[pl.ds(g * 16, 16)]
         return carry
 
-    zeroth, first, second, third, fourth = [], [], [], [], []
+    zeroth, first, second, third = [], [], [], []
     for k, (a1, a2, a3) in enumerate(orders):
         lax.fori_loop(*part_blocks(c, k), block, 0)
         core_waits[k].wait_recv()
@@ -472,27 +476,36 @@
                 lambda q, row=row, k=k: out.at[pl.ds(row + q * n2[k], n2[k])],
             )
         )
-    lax.fori_loop(cuts[2], cuts[3], pivot, 0)
-    for k, (a1, a2, a3) in enumerate(orders):
-        third[k]()
-        row = base[k] + place[a1] * n1[k]
-        fourth.append(
+    def last(k, n):
+        a1, a2, a3 = orders[k]
+        spot = around(place[a2], 4 - n) * n2[k]
+        fourth[k].append(
             spread(
-                16 + k, a1,
-                lambda q, row=row, k=k: out.at[pl.ds(row, n1[k])],
-                lambda q, k=k: out.at[pl.ds(base[k] + q * n1[k], n1[k])],
+                22 + 4 * k + n, a1,
+                lambda q: out.at[pl.ds(base[k] + place[a1] * n1[k] + spot, n2[k])],
+                lambda q: out.at[pl.ds(base[k] + q * n1[k] + spot, n2[k])],
             )
         )
+
+    fourth = [[], [], []]
+    for k in range(3):
+        last(k, 0)
+    lax.fori_loop(cuts[2], cuts[3], pivot, 0)
+    for n in (1, 3, 2):
+        for k in range(3):
+            third[k]((n,))
+            last(k, n)
     lax.fori_loop(cuts[3], cuts[4], pivot, 0)
     m = M[...]
     diag = jnp.sum(jnp.where(lane_id == row_id, m, 0.0), axis=1, keepdims=True)
     linv = pltpu.roll(m / jnp.sqrt(diag), rank, 1)[:, 0:rank]
-    ortho_out[...] = jnp.dot(linv, (L1[0] + L1[1] + L1[2] + L1[3]) * (1.0 / 8.0), precision=HI, preferred_element_type=f32)
+    ortho_out[...] = jnp.dot(linv, LF[...], precision=HI, preferred_element_type=f32)
     v_high, v_low = split(linv * (1.0 / 8.0))
     LV[0] = v_high
     LV[1] = v_low
     for k in range(3):
-        fourth[k]()
+        for done in fourth[k]:
+            done()
         r = pl.ds(base[k], sizes[k])
         swap(20, out.at[r], out.at[r], k)
 
@@ -560,8 +573,9 @@
             VMEM((2 * rank, cols), bf16),
             VMEM((rank, cols), f32),
             VMEM((rank, rows), f32),
+            VMEM((rank // 2, rows), f32),
+            VMEM((4, rank // 2, rows), f32),
             VMEM((rank, rows), f32),
-            VMEM((4, rank, rows), f32),
             VMEM((2 * rank, rows), bf16),
             VMEM((2, rank, rank), bf16),
             VMEM((tiles, 8, 128), f32),
@@ -576,7 +590,7 @@
             DMA((5,)), DMA((6,)), DMA((6,)), DMA((6,)), DMA((6,)),
             DMA((4, 4)), DMA((4, 4)), DMA((4, 4)), DMA((4, 4)),
             DMA((2, 2)), DMA((2, 2)), DMA((2, 2)), DMA((2, 2)),
-            DMA((21, 4)), DMA((21, 4)),
+            DMA((34, 4)), DMA((34, 4)),
         ],
         compiler_params=pltpu.CompilerParams(
             collective_id=0, has_side_effects=True, vmem_limit_bytes=COMM_BYTES

time: 126 us -> 126 us (level)
  no operation moved by 1% of the time
where the time goes in v6:
time: 126 us
  Pallas kernels  126 us (100%)
    pallas_call x1, Pallas kernels, communicate(): pl.pallas_call(comm_kernel, out_shape=(jax.ShapeDtypeStruct((rows, cols),...  121 us
    pallas_call x1, Pallas kernels, finish(): pl.pallas_call(functools.partial(finish_kernel, coef), out_shape=(jax.Sha...  4.2 us

profile of v6, /device:TPU:1, one launch (start us, length us, event | category | flops | bytes accessed | tf_op | source)
XLA Modules:
  0.0 126.3 jit_solution(8253516461368499130)
XLA Ops:
  0.6 0.0 copy-start
  0.6 121.4 %communicate.1 = (f32[256,5120]{1,0:T(8,128)S(1)}, f32[64,5120]{1,0:T(8,128)S(1)}, f32[64,128]{1,0:T(8,128)S(1)}, f32[64,256]{1,0:T(8,128)S(1)}) custom-call(bf16[3072,256]{1,0:T(8,128)(2,1)} %cot.1, bf16[320,3072]{1,0:T(8,128)(2,1)} %bitcast.6, s32[8]{0:T(128)} %lengths.1, f32[256,5120]{1,0:T(8,128)} %bitcast.5, f32[64,5120]{1,0:T(8,128)} %bitcast.7), custom_call_target="tpu_custom_call" | custom-call | tf_op jit(solution)/shard_map/communicate/pallas_call | solution.py:551
  122.0 0.0 copy-done
  122.1 4.2 %finish.1 = (bf16[256,5120]{1,0:T(8,128)(2,1)}, f32[256,5120]{1,0:T(8,128)}, f32[64,5120]{1,0:T(8,128)}) custom-call(f32[64,5120]{1,0:T(8,128)S(1)} %get-tuple-element.10.right_t, f32[64,128]{1,0:T(8,128)S(1)} %get-tuple-element.11.norm, f32[64,256]{1,0:T(8,128)S(1)} %get-tuple-element.12.ortho_t, f32[256,5120]{1,0:T(8,128)S(1)} %get-tuple-element.13.both, ...), custom_call_target="tpu_custom_call" | custom-call | tf_op jit(solution)/shard_map/finish/pallas_call | solution.py:642
Async XLA Ops:
  0.6 121.4 %copy-start = (bf16[256,5120]{1,0:T(8,128)(2,1)S(1)}, bf16[256,5120]{1,0:T(8,128)(2,1)}, u32[]{:S(2)}) copy-start(bf16[256,5120]{1,0:T(8,128)(2,1)} %weight.1) | copy-start | bytes 7864324

commit v7 on v5

--- a/solution.py
+++ b/solution.py
@@ -20,7 +20,7 @@
 CODES = 32767.0
 COMM_BYTES = 38 * 2**20
 FINISH_BYTES = 16 * 2**20
-DEPTH = 768
+DEPTH = 1536
 
 
 def vspec():
@@ -119,6 +119,8 @@
         pltpu.make_async_copy(mom, both, sl.at[2]),
         pltpu.make_async_copy(rft, rfv, sl.at[3]),
     ]
+    for copy in locals_:
+        copy.start()
     greet([mate] + [along(a, around(place[a], q)) for a in "xyz" for q in (1, 2, 3)])
 
     def part_a(h):
@@ -135,8 +137,6 @@
         cb = remote(bt.at[part_b(half)], B.at[pb, part_b(half)], sb.at[k], rb.at[k], along("b", br if right else bl))
         cb.start()
         sent += [ca, cb]
-    for copy in locals_:
-        copy.start()
 
     def got_a(k):
         remote(A.at[pa, part_a(0)], A.at[pa, part_a(0)], sa.at[0], ra.at[k], along("a", ar)).wait_recv()

time: 126 us -> 126 us (level)
  no operation moved by 1% of the time
where the time goes in v7:
time: 126 us; the launch traced here: 125 us
  Pallas kernels  125 us (99%)
    pallas_call x1, Pallas kernels, communicate(): pl.pallas_call(comm_kernel, out_shape=(jax.ShapeDtypeStruct((rows, cols),...  121 us
    pallas_call x1, Pallas kernels, finish(): pl.pallas_call(functools.partial(finish_kernel, coef), out_shape=(jax.Sha...  4.2 us

profile of v7, /device:TPU:1, one launch (start us, length us, event | category | flops | bytes accessed | tf_op | source)
XLA Modules:
  0.0 125.4 jit_solution(3556085970477569874)
XLA Ops:
  0.6 0.0 copy-start
  0.6 120.5 %communicate.1 = (f32[256,5120]{1,0:T(8,128)S(1)}, f32[64,5120]{1,0:T(8,128)S(1)}, f32[64,128]{1,0:T(8,128)S(1)}, f32[64,256]{1,0:T(8,128)S(1)}) custom-call(bf16[3072,256]{1,0:T(8,128)(2,1)} %cot.1, bf16[320,3072]{1,0:T(8,128)(2,1)} %bitcast.6, s32[8]{0:T(128)} %lengths.1, f32[256,5120]{1,0:T(8,128)} %bitcast.5, f32[64,5120]{1,0:T(8,128)} %bitcast.7), custom_call_target="tpu_custom_call" | custom-call | tf_op jit(solution)/shard_map/communicate/pallas_call | solution.py:538
  121.2 0.0 copy-done
  121.2 4.2 %finish.1 = (bf16[256,5120]{1,0:T(8,128)(2,1)}, f32[256,5120]{1,0:T(8,128)}, f32[64,5120]{1,0:T(8,128)}) custom-call(f32[64,5120]{1,0:T(8,128)S(1)} %get-tuple-element.10.right_t, f32[64,128]{1,0:T(8,128)S(1)} %get-tuple-element.11.norm, f32[64,256]{1,0:T(8,128)S(1)} %get-tuple-element.12.ortho_t, f32[256,5120]{1,0:T(8,128)S(1)} %get-tuple-element.13.both, ...), custom_call_target="tpu_custom_call" | custom-call | tf_op jit(solution)/shard_map/finish/pallas_call | solution.py:628
Async XLA Ops:
  0.6 120.6 %copy-start = (bf16[256,5120]{1,0:T(8,128)(2,1)S(1)}, bf16[256,5120]{1,0:T(8,128)(2,1)}, u32[]{:S(2)}) copy-start(bf16[256,5120]{1,0:T(8,128)(2,1)} %weight.1) | copy-start | bytes 7864324
